TPU v7x, 256 devices: a whole 4x4x8 slice. The times are simulated.
256 devices in a mesh: tm: 16 (over x, z_lo), py: 4 (over y), pz: 4 (over z_hi, core).
Axes of the slice: x: 4, y: 4, z: 8 (z_hi: 2, z_lo: 4; z = z_hi * 4 + z_lo), core: 2. Of those that a mesh axis runs over, the one named last changes fastest.
Arguments:
- start_states: float32 [16, 3, 128, 8, 16, 128], P('tm', None, None, None, ('py', 'pz')), may hold values from -6 to 6
Outputs:
- new_states: float32 [16, 3, 128, 8, 16, 128], P('tm', None, None, None, ('py', 'pz'))
All inputs are finite; a program needn't handle non-finite values.
Results may differ from a plain program's by a relative error of at most 0.0001.
Values sent between devices are 32-bit elements; how exact they have to be, the bound alone decides.
A program may use at most 128 MiB of HBM per device.

v0:
```python
from functools import partial
import math

import jax
import jax.numpy as jnp
from jax import lax
from jax.sharding import PartitionSpec as P

M = 64


viscosity = 0.03
time_step = 0.004
highest = lax.Precision.HIGHEST


def items_in_groups(x, axis, split_dim, concat_dim, work, item_dim, out_dim):

    def moved(group):
        return lax.all_to_all(group, axis, split_axis=split_dim, concat_axis=concat_dim, tiled=True)

    items = jax.tree.leaves(x)[0].shape[item_dim]
    ends = [items * k // 2 for k in range(2 + 1)] if items % 2 == 0 else [0, items]
    groups = [
        jax.tree.map(lambda a: lax.slice_in_dim(a, low, high, axis=item_dim), x)
        for low, high in zip(ends, ends[1:])
    ]
    arrived = [moved(group) for group in groups]
    made = [work(group) for group in arrived]
    return jax.tree.map(lambda *parts: jnp.concatenate(parts, axis=out_dim), *made)


def shifted(block, axis, distance):
    devices = range(lax.axis_size(axis))
    route = [(i - distance, i) for i in devices if i - distance in devices]
    return lax.ppermute(block, axis, route)


def signed_wave(places, length):
    return jnp.where(places < length // 2, places, places - length)


def rotate(values):
    halfway = values.shape[-1] // 2
    return jnp.concatenate([-values[..., halfway:], values[..., :halfway]], axis=-1)


def trig_pair(outer, inner, extent, factor):
    residue = jnp.mod(outer[:, None] * inner[None, :], extent)
    radians = residue.astype(jnp.float32) * (2.0 * math.pi / extent)
    return (jnp.cos(radians) * factor, jnp.sin(radians) * factor)


def complex_apply(cosine_part, sine_part, values, contracted, direction_sign):
    kernel = jnp.stack(
        [
            jnp.stack([cosine_part, -direction_sign * sine_part]),
            jnp.stack([direction_sign * sine_part, cosine_part]),
        ]
    )
    halfway = values.shape[-1] // 2
    split = values.reshape(values.shape[:-1] + (2, halfway))
    if contracted == 1:
        pattern = "pqok,fkaqh->foaph"
    else:
        pattern = "pqok,flkqh->floph"
    result = jnp.einsum(pattern, kernel, split, precision=highest)
    return result.reshape(result.shape[:-2] + (2 * halfway,))


def inverse_z(extent, retained):
    halfway = retained // 2
    columns = jnp.arange(retained, dtype=jnp.int32)
    harmonic = columns % halfway
    weight = jnp.where(harmonic == 0, 1.0, 2.0) * retained ** (-0.5)
    residue = jnp.mod(harmonic[:, None] * jnp.arange(extent, dtype=jnp.int32)[None, :], extent)
    radians = residue.astype(jnp.float32) * (2.0 * math.pi / extent)
    return (
        jnp.where((columns < halfway)[:, None], jnp.cos(radians), -jnp.sin(radians))
        * weight[:, None]
    )


def forward_z(extent, retained):
    halfway = retained // 2
    columns = jnp.arange(retained, dtype=jnp.int32)
    harmonic = columns % halfway
    residue = jnp.mod(jnp.arange(extent, dtype=jnp.int32)[:, None] * harmonic[None, :], extent)
    radians = residue.astype(jnp.float32) * (2.0 * math.pi / extent)
    return jnp.where((columns < halfway)[None, :], jnp.cos(radians), -jnp.sin(radians)) * (
        math.sqrt(retained) / extent
    )


def inverse_tail(portion, extent, sectioned, layout):
    count_py, count_pz, groups, member = layout
    retained = portion.shape[2]
    local_rows = retained // groups
    places = jnp.arange(retained, dtype=jnp.int32)
    owners = places // local_rows
    wave_y = signed_wave(places % local_rows * groups + owners, retained)
    points = jnp.arange(extent, dtype=jnp.int32)
    cosine_part, sine_part = trig_pair(points, wave_y, extent, retained ** (-0.5))
    along_y = complex_apply(cosine_part, sine_part, portion, 2, 1.0)
    return jnp.einsum("flyr,rz->flyz", along_y, inverse_z(extent, retained), precision=highest)


def forward_tail(portion, retained, sectioned, layout):
    count_py, count_pz, groups, member = layout
    extent = portion.shape[1]
    local_rows = extent // groups
    places = jnp.arange(extent, dtype=jnp.int32)
    points = places // local_rows * local_rows + places % local_rows
    wave_x = signed_wave(jnp.arange(retained, dtype=jnp.int32), retained)
    cosine_part, sine_part = trig_pair(wave_x, points, extent, math.sqrt(retained) / extent)
    return complex_apply(cosine_part, sine_part, portion, 1, -1.0)


def to_physical(coeffs, wavegrid, extent, resolution, layout):
    wave_x, wave_y, wave_z = wavegrid
    retained = coeffs.shape[1]
    seeds = jnp.concatenate([coeffs, wave_x * coeffs[1:3]], axis=0)
    points = jnp.arange(extent, dtype=jnp.int32)
    wave_rows = signed_wave(jnp.arange(retained, dtype=jnp.int32), retained)
    cosine_part, sine_part = trig_pair(points, wave_rows, extent, retained ** (-0.5))
    moved_x = complex_apply(cosine_part, sine_part, seeds, 1, 1.0)
    curl_x = rotate(wave_y * moved_x[2] - wave_z * moved_x[1])
    curl_y = rotate(wave_z * moved_x[0] - moved_x[4])
    curl_z = rotate(moved_x[3] - wave_y * moved_x[0])
    spread = jnp.concatenate([moved_x[:3], jnp.stack([curl_x, curl_y, curl_z])], axis=0)
    if resolution == "coarse":
        finish = partial(inverse_tail, extent=extent, sectioned=False, layout=layout)
        return finish(lax.all_to_all(spread, ("py", "pz"), split_axis=1, concat_axis=2, tiled=True))
    else:
        finish = partial(inverse_tail, extent=extent, sectioned=False, layout=layout)
        return items_in_groups(spread, ("py", "pz"), 1, 2, finish, 0, 0)


def to_spectral(fields, retained, resolution, layout):
    count_py, count_pz, groups, member = layout
    extent = fields.shape[-1]
    along_z = jnp.einsum("flyz,zr->flyr", fields, forward_z(extent, retained), precision=highest)
    local_rows = retained // groups
    places = jnp.arange(retained, dtype=jnp.int32)
    wave_y = signed_wave(places % local_rows * groups + places // local_rows, retained)
    cosine_part, sine_part = trig_pair(
        wave_y, jnp.arange(extent, dtype=jnp.int32), extent, math.sqrt(retained) / extent
    )
    along_y = complex_apply(cosine_part, sine_part, along_z, 2, -1.0)
    if resolution == "coarse":
        finish = partial(forward_tail, retained=retained, sectioned=False, layout=layout)
        return finish(
            lax.all_to_all(along_y, ("py", "pz"), split_axis=2, concat_axis=1, tiled=True)
        )
    else:
        finish = partial(forward_tail, retained=retained, sectioned=False, layout=layout)
        return finish(
            lax.all_to_all(along_y, ("py", "pz"), split_axis=2, concat_axis=1, tiled=True)
        )


def wave_grid(retained, layout):
    count_py, count_pz, groups, member = layout
    places = jnp.arange(retained, dtype=jnp.int32)
    wave_x = signed_wave(places, retained).astype(jnp.float32)[:, None, None]
    local_places = jnp.arange(retained // groups, dtype=jnp.int32)
    wave_y = signed_wave(local_places * groups + member, retained).astype(jnp.float32)[
        None, :, None
    ]
    wave_z = (places % (retained // 2)).astype(jnp.float32)[None, None, :]
    return (wave_x, wave_y, wave_z)


def project(coeffs, wavegrid):
    wave_x, wave_y, wave_z = wavegrid
    squared = wave_x * wave_x + wave_y * wave_y + wave_z * wave_z
    divergence = (wave_x * coeffs[0] + wave_y * coeffs[1] + wave_z * coeffs[2]) / jnp.maximum(
        squared, 1.0
    )
    return jnp.stack(
        [
            coeffs[0] - wave_x * divergence,
            coeffs[1] - wave_y * divergence,
            coeffs[2] - wave_z * divergence,
        ]
    )


def cross_product(first_field, second_field):
    return jnp.stack(
        [
            first_field[1] * second_field[2] - first_field[2] * second_field[1],
            first_field[2] * second_field[0] - first_field[0] * second_field[2],
            first_field[0] * second_field[1] - first_field[1] * second_field[0],
        ]
    )


def advance(coeffs, resolution, layout):
    retained = coeffs.shape[1]
    extent = 3 * retained // 2
    wavegrid = wave_grid(retained, layout)
    fields = to_physical(coeffs, wavegrid, extent, resolution, layout)
    product = cross_product(fields[:3], fields[3:])
    nonlinear = to_spectral(product, retained, resolution, layout)
    wave_x, wave_y, wave_z = wavegrid
    squared = wave_x * wave_x + wave_y * wave_y + wave_z * wave_z
    damping = jnp.exp(-viscosity * time_step * squared)
    return damping * (coeffs + time_step * project(nonlinear, wavegrid))


def restrict(coeffs, kept, groups):
    halfway = kept // 2
    retained = coeffs.shape[1]
    rows_kept = jnp.concatenate([coeffs[:, :halfway], coeffs[:, retained - halfway :]], axis=1)
    local_rows = coeffs.shape[2]
    local_kept = kept // groups // 2
    rows_kept = jnp.concatenate(
        [rows_kept[:, :, :local_kept], rows_kept[:, :, local_rows - local_kept :]], axis=2
    )
    columns_half = coeffs.shape[3] // 2
    return jnp.concatenate(
        [rows_kept[..., :halfway], rows_kept[..., columns_half : columns_half + halfway]], axis=3
    )


def prolong(coeffs, retained, groups):
    components, kept, local_kept, width = coeffs.shape
    halfway = kept // 2
    zeros_x = jnp.zeros((components, retained - kept, local_kept, width), jnp.float32)
    wider = jnp.concatenate([coeffs[:, :halfway], zeros_x, coeffs[:, halfway:]], axis=1)
    local_rows = retained // groups
    split_rows = local_kept // 2
    zeros_y = jnp.zeros((components, retained, local_rows - local_kept, width), jnp.float32)
    wider = jnp.concatenate([wider[:, :, :split_rows], zeros_y, wider[:, :, split_rows:]], axis=2)
    zeros_z = jnp.zeros((components, retained, local_rows, retained // 2 - halfway), jnp.float32)
    return jnp.concatenate([wider[..., :halfway], zeros_z, wider[..., halfway:], zeros_z], axis=3)


def shards(start_states):
    count_py = lax.axis_size("py")
    count_pz = lax.axis_size("pz")
    groups = count_py * count_pz
    member = lax.axis_index("py") * count_pz + lax.axis_index("pz")
    layout = (count_py, count_pz, groups, member)
    position = lax.axis_index("tm")
    slices = lax.axis_size("tm")
    retained = start_states.shape[-1]
    stored = start_states.reshape(3, retained, start_states.shape[3], retained)
    spectral_state = project(stored, wave_grid(retained, layout))
    fine_end = advance(spectral_state, "fine", layout)
    coarse_start = restrict(spectral_state, M, groups)
    coarse_next = advance(coarse_start, "coarse", layout)
    fine_low = restrict(fine_end, M, groups)
    correction = fine_low - coarse_next
    payload = jnp.where(position == 0, fine_low, correction)
    everything = lax.all_gather(payload[None], "tm", axis=0, tiled=True)

    def sweep_turn(turn_index, carried):
        chained, current = carried
        chained = advance(chained, "coarse", layout) + lax.dynamic_index_in_dim(
            everything, turn_index, 0, keepdims=False
        )
        return (chained, jnp.where(position == turn_index + 1, chained, current))

    start_value = everything[0]
    chained, current = lax.fori_loop(
        1,
        slices - 1,
        sweep_turn,
        (start_value, jnp.where(position == 1, start_value, coarse_start)),
    )
    upper_band = fine_end - prolong(fine_low, retained, groups)
    previous = shifted(upper_band, "tm", 1)
    updated = prolong(current, retained, groups) + previous
    result = jnp.where(position == 0, spectral_state, updated)
    return result.reshape(1, result.shape[0], retained, result.shape[2], 1, retained)


def solution(mesh):
    in_specs = (P("tm", None, None, None, ("py", "pz"), None),)
    out_specs = P("tm", None, None, None, ("py", "pz"), None)
    return jax.shard_map(shards, mesh=mesh, in_specs=in_specs, out_specs=out_specs, check_vma=False)
```

profile of v0, /device:TPU:103, one launch (start us, length us, event | category | flops | bytes accessed | tf_op | source)
XLA Modules:
  0.0 1607.6 jit_solution(7569490869302460713)
XLA Ops:
  33.1 9.1 all-to-all-start.3
  46.1 37.8 %all-to-all-done.3 = f32[3,192,8,128]{3,2,0,1:T(8,128)} async-done(((f32[3,192,8,128]{3,2,0,1:T(8,128)}), f32[3,192,8,128]{3,2,0,1:T(8,128)}, u32[]{:S(2)}, u32[]{:S(2)}) %all-to-all-start.3) | async-done | bytes 2359328 | tf_op jit(solution)/shard_map/all_to_all | solution.py:20
  84.0 21.8 %all-to-all-start.2 = ((f32[3,192,8,128]{3,2,0,1:T(8,128)}), f32[3,192,8,128]{3,2,0,1:T(8,128)}, u32[]{:S(2)}, u32[]{:S(2)}) async-start(f32[3,192,8,128]{3,2,0,1:T(8,128)} %copy.201), calls=%async_computation.2 | async-start | bytes 4718592 | tf_op jit(solution)/shard_map/all_to_all | solution.py:20
  112.8 31.4 %all-to-all-done.2 = f32[3,192,8,128]{3,2,0,1:T(8,128)} async-done(((f32[3,192,8,128]{3,2,0,1:T(8,128)}), f32[3,192,8,128]{3,2,0,1:T(8,128)}, u32[]{:S(2)}, u32[]{:S(2)}) %all-to-all-start.2) | async-done | bytes 2359328 | tf_op jit(solution)/shard_map/all_to_all | solution.py:20
  150.4 17.6 %fusion.126 = f32[3,12,64,2,192,1]{4,2,5,3,1,0:T(8,128)S(1)} fusion(f32[3,12,128,2,64,1]{4,3,2,1,0,5:T(2,128)} %bitcast.518, f32[1,2,192,128]{3,2,1,0:T(8,128)S(1)} %get-tuple-element.472, f32[1,2,192,128]{3,2,1,0:T(8,128)S(1)} %get-tuple-element.471), kind=kOutput, calls=%fused_computation.195 | convolution fusion | flops 2718007296 | bytes 6291456 | tf_op jit(solution)/shard_map/pqok,flkqh->floph/dot_general | solution.py:67
  168.0 15.2 fusion.128
  183.2 8.3 fusion.195
  191.5 8.5 fusion.197
  204.0 12.0 fusion.118
  222.9 25.4 %all-to-all-start.4 = ((f32[3,12,128,128]{3,1,0,2:T(8,128)}), f32[3,12,128,128]{3,1,0,2:T(8,128)S(1)}, u32[]{:S(2)}, u32[]{:S(2)}) async-start(f32[3,12,128,128]{3,1,0,2:T(8,128)} %copy.219), calls=%async_computation.4 | async-start | bytes 6291456 | tf_op jit(solution)/shard_map/all_to_all | solution.py:158
  256.1 68.3 %all-to-all-done.4 = f32[3,12,128,128]{3,1,0,2:T(8,128)S(1)} async-done(((f32[3,12,128,128]{3,1,0,2:T(8,128)}), f32[3,12,128,128]{3,1,0,2:T(8,128)S(1)}, u32[]{:S(2)}, u32[]{:S(2)}) %all-to-all-start.4) | async-done | bytes 2359328 | tf_op jit(solution)/shard_map/all_to_all | solution.py:158
  332.7 10.3 fusion.148
  368.9 12.2 all-to-all-done.5
  411.6 10.1 all-to-all-done.6
  433.3 136.7 %all-gather.2.cloned.1.call-done = f32[16,3,64,4,64]{4,2,3,1,0:T(8,128)} async-done(((f32[1,3,64,4,64]{4,2,3,1,0:T(8,128)}), f32[16,3,64,4,64]{4,2,3,1,0:T(8,128)}) %all-gather.2.cloned.1.call-update) | async-done | bytes 3145744 | tf_op jit(solution)/shard_map/all_gather | solution.py:257
  573.3 978.9 %while.19 = (s32[]{:T(128)}, f32[3,64,4,64]{1,3,2,0:T(8,128)S(1)}, f32[3,64,4,64]{1,3,2,0:T(8,128)}, s32[]{:T(128)}, f32[16,3,64,4,64]{4,2,3,1,0:T(8,128)}, /*in...) while((s32[]{:T(128)}, f32[3,64,4,64]{1,3,2,0:T(8,128)S(1)}, ...), condition=%wide.region_1.2_spmd, body=%wide.region_0.1_spmd.sunk | while | flops 1196723456 | bytes 40041012 | solution.py:267
  579.5 11.0 all-to-all-start
  596.7 12.0 all-to-all-done
  631.1 11.2 all-to-all-done.1
  666.4 8.2 all-to-all-done
  700.3 11.2 all-to-all-done.1
  761.4 8.1 all-to-all-start.1
  769.7 11.2 all-to-all-done.1
  805.3 8.1 all-to-all-done
  830.8 8.1 all-to-all-start.1
  839.1 11.2 all-to-all-done.1
  874.7 8.1 all-to-all-done
  900.2 8.1 all-to-all-start.1
  908.6 11.2 all-to-all-done.1
  969.7 8.1 all-to-all-start.1
  978.0 11.2 all-to-all-done.1
  1039.1 8.1 all-to-all-start.1
  1047.5 11.2 all-to-all-done.1
  1108.6 8.1 all-to-all-start.1
  1116.9 11.2 all-to-all-done.1
  1178.0 8.1 all-to-all-start.1
  1186.3 11.2 all-to-all-done.1
  1247.4 8.1 all-to-all-start.1
  1255.8 11.2 all-to-all-done.1
  1316.9 8.1 all-to-all-start.1
  1325.2 11.2 all-to-all-done.1
  1386.3 8.1 all-to-all-start.1
  1394.7 11.2 all-to-all-done.1
  1455.8 8.1 all-to-all-start.1
  1464.1 11.2 all-to-all-done.1
  1525.2 8.1 all-to-all-start.1
  1533.5 11.2 all-to-all-done.1
  1560.1 36.3 %collective-permute-done = f32[3,128,8,128]{3,1,2,0:T(8,128)S(1)} collective-permute-done((f32[3,128,8,128]{3,1,2,0:T(8,128)S(1)}, f32[3,128,8,128]{3,1,2,0:T(8,128)S(1)}, u32[]{:S(2)}, u32[]{:S(2)}) %collective-permute-start) | collective-permute-done | bytes 1572896 | tf_op jit(solution)/shard_map/ppermute | solution.py:36
  (1620 shorter events, 822.8 us)
Async XLA Ops:
  6.6 21.4 %copy-start.61 = (f32[128]{0:T(128)}, f32[128]{0:T(128)S(1)}, u32[]{:S(2)}) copy-start(f32[128]{0:T(128)S(1)} %fusion.329) | copy-start | bytes 1540
  33.1 50.9 %all-to-all-start.3 = ((f32[3,192,8,128]{3,2,0,1:T(8,128)}), f32[3,192,8,128]{3,2,0,1:T(8,128)}, u32[]{:S(2)}, u32[]{:S(2)}) async-start(f32[3,192,8,128]{3,2,0,1:T(8,128)} %pad_maximum_fusion.2), calls=%async_computation.3 | async-start | bytes 4718592 | tf_op jit(solution)/shard_map/all_to_all | solution.py:20
  84.0 60.3 %all-to-all-start.2 = ((f32[3,192,8,128]{3,2,0,1:T(8,128)}), f32[3,192,8,128]{3,2,0,1:T(8,128)}, u32[]{:S(2)}, u32[]{:S(2)}) async-start(f32[3,192,8,128]{3,2,0,1:T(8,128)} %copy.201), calls=%async_computation.2 | async-start | bytes 4718592 | tf_op jit(solution)/shard_map/all_to_all | solution.py:20
  150.4 17.6 %copy-start.5 = (f32[3,12,128,2,64]{4,3,2,1,0:T(2,128)S(1)}, f32[3,12,128,2,64]{4,3,2,1,0:T(2,128)}, u32[]{:S(2)}) copy-start(f32[3,12,128,2,64]{4,3,2,1,0:T(2,128)} %reshape.3223) | copy-start | bytes 7077892
  222.9 101.5 %all-to-all-start.4 = ((f32[3,12,128,128]{3,1,0,2:T(8,128)}), f32[3,12,128,128]{3,1,0,2:T(8,128)S(1)}, u32[]{:S(2)}, u32[]{:S(2)}) async-start(f32[3,12,128,128]{3,1,0,2:T(8,128)} %copy.219), calls=%async_computation.4 | async-start | bytes 6291456 | tf_op jit(solution)/shard_map/all_to_all | solution.py:158
  347.7 62.7 %copy-start.8 = (f32[3,128,8,128]{3,1,2,0:T(8,128)}, f32[3,128,8,128]{3,1,2,0:T(8,128)S(1)}, u32[]{:S(2)}) copy-start(f32[3,128,8,128]{3,1,2,0:T(8,128)S(1)} %get-tuple-element.415) | copy-start | bytes 4718596
  358.5 9.7 copy-start.53
  360.4 20.7 %all-to-all-start.5 = ((f32[16,1,9216]{2,1,0:T(1,128)}), f32[16,1,9216]{2,1,0:T(1,128)S(1)}, u32[]{:S(2)}, u32[]{:S(2)}) async-start(f32[16,1,9216]{2,1,0:T(1,128)} %reshape.3285), calls=%async_computation.5 | async-start | bytes 1179648 | tf_op jit(solution)/shard_map/all_to_all | solution.py:133
  405.7 16.1 all-to-all-start.6
  410.4 159.7 %all-gather.2.cloned.1.call-start = ((), (), s32[]{:S(2)}) async-start(), calls=%async_computation.7 | async-start | bytes 6684672 | tf_op jit(solution)/shard_map/all_gather | solution.py:257
  411.6 20.9 %copy-start.27 = (f32[3,64,4,32]{3,1,2,0:T(8,128)}, f32[3,64,4,32]{3,1,2,0:T(8,128)S(1)}, u32[]{:S(2)}) copy-start(f32[3,64,4,32]{3,1,2,0:T(8,128)S(1)} %get-tuple-element.457) | copy-start | bytes 294916
  411.6 20.9 %copy-start.29 = (f32[3,64,4,32]{3,1,2,0:T(8,128)}, f32[3,64,4,32]{3,1,2,0:T(8,128)S(1)}, u32[]{:S(2)}) copy-start(f32[3,64,4,32]{3,1,2,0:T(8,128)S(1)} %get-tuple-element.458) | copy-start | bytes 294916
  579.5 29.2 %all-to-all-start = ((f32[16,1,9216]{2,1,0:T(1,128)}), f32[16,1,9216]{2,1,0:T(1,128)S(1)}, u32[]{:S(2)}, u32[]{:S(2)}) async-start(f32[16,1,9216]{2,1,0:T(1,128)} %reshape.3295), calls=%async_computation | async-start | bytes 1179648 | tf_op jit(solution)/shard_map/while/body/eval_jaxpr/all_to_all | solution.py:133
  626.2 16.1 %all-to-all-start.1 = ((f32[16,1,4608]{2,1,0:T(1,128)}), f32[16,1,4608]{2,1,0:T(1,128)S(1)}, u32[]{:S(2)}, u32[]{:S(2)}) async-start(f32[16,1,4608]{2,1,0:T(1,128)} %reshape.3298), calls=%async_computation.1 | async-start | bytes 589824 | tf_op jit(solution)/shard_map/while/body/eval_jaxpr/all_to_all | solution.py:153
  655.6 18.9 %all-to-all-start = ((f32[16,1,9216]{2,1,0:T(1,128)}), f32[16,1,9216]{2,1,0:T(1,128)S(1)}, u32[]{:S(2)}, u32[]{:S(2)}) async-start(f32[16,1,9216]{2,1,0:T(1,128)} %reshape.3295), calls=%async_computation | async-start | bytes 1179648 | tf_op jit(solution)/shard_map/while/body/eval_jaxpr/all_to_all | solution.py:133
  692.0 19.4 %all-to-all-start.1 = ((f32[16,1,4608]{2,1,0:T(1,128)}), f32[16,1,4608]{2,1,0:T(1,128)S(1)}, u32[]{:S(2)}, u32[]{:S(2)}) async-start(f32[16,1,4608]{2,1,0:T(1,128)} %reshape.3298), calls=%async_computation.1 | async-start | bytes 589824 | tf_op jit(solution)/shard_map/while/body/eval_jaxpr/all_to_all | solution.py:153
  724.7 19.2 %all-to-all-start = ((f32[16,1,9216]{2,1,0:T(1,128)}), f32[16,1,9216]{2,1,0:T(1,128)S(1)}, u32[]{:S(2)}, u32[]{:S(2)}) async-start(f32[16,1,9216]{2,1,0:T(1,128)} %reshape.3295), calls=%async_computation | async-start | bytes 1179648 | tf_op jit(solution)/shard_map/while/body/eval_jaxpr/all_to_all | solution.py:133
  761.4 19.5 %all-to-all-start.1 = ((f32[16,1,4608]{2,1,0:T(1,128)}), f32[16,1,4608]{2,1,0:T(1,128)S(1)}, u32[]{:S(2)}, u32[]{:S(2)}) async-start(f32[16,1,4608]{2,1,0:T(1,128)} %reshape.3298), calls=%async_computation.1 | async-start | bytes 589824 | tf_op jit(solution)/shard_map/while/body/eval_jaxpr/all_to_all | solution.py:153
  794.1 19.2 %all-to-all-start = ((f32[16,1,9216]{2,1,0:T(1,128)}), f32[16,1,9216]{2,1,0:T(1,128)S(1)}, u32[]{:S(2)}, u32[]{:S(2)}) async-start(f32[16,1,9216]{2,1,0:T(1,128)} %reshape.3295), calls=%async_computation | async-start | bytes 1179648 | tf_op jit(solution)/shard_map/while/body/eval_jaxpr/all_to_all | solution.py:133
  829.3 9.6 copy-start.48
  829.3 9.6 copy-start.49
  830.8 19.5 %all-to-all-start.1 = ((f32[16,1,4608]{2,1,0:T(1,128)}), f32[16,1,4608]{2,1,0:T(1,128)S(1)}, u32[]{:S(2)}, u32[]{:S(2)}) async-start(f32[16,1,4608]{2,1,0:T(1,128)} %reshape.3298), calls=%async_computation.1 | async-start | bytes 589824 | tf_op jit(solution)/shard_map/while/body/eval_jaxpr/all_to_all | solution.py:153
  863.6 19.2 %all-to-all-start = ((f32[16,1,9216]{2,1,0:T(1,128)}), f32[16,1,9216]{2,1,0:T(1,128)S(1)}, u32[]{:S(2)}, u32[]{:S(2)}) async-start(f32[16,1,9216]{2,1,0:T(1,128)} %reshape.3295), calls=%async_computation | async-start | bytes 1179648 | tf_op jit(solution)/shard_map/while/body/eval_jaxpr/all_to_all | solution.py:133
  898.8 9.6 copy-start.48
  898.8 9.6 copy-start.49
  900.2 19.5 %all-to-all-start.1 = ((f32[16,1,4608]{2,1,0:T(1,128)}), f32[16,1,4608]{2,1,0:T(1,128)S(1)}, u32[]{:S(2)}, u32[]{:S(2)}) async-start(f32[16,1,4608]{2,1,0:T(1,128)} %reshape.3298), calls=%async_computation.1 | async-start | bytes 589824 | tf_op jit(solution)/shard_map/while/body/eval_jaxpr/all_to_all | solution.py:153
  933.0 19.2 %all-to-all-start = ((f32[16,1,9216]{2,1,0:T(1,128)}), f32[16,1,9216]{2,1,0:T(1,128)S(1)}, u32[]{:S(2)}, u32[]{:S(2)}) async-start(f32[16,1,9216]{2,1,0:T(1,128)} %reshape.3295), calls=%async_computation | async-start | bytes 1179648 | tf_op jit(solution)/shard_map/while/body/eval_jaxpr/all_to_all | solution.py:133
  969.7 19.5 %all-to-all-start.1 = ((f32[16,1,4608]{2,1,0:T(1,128)}), f32[16,1,4608]{2,1,0:T(1,128)S(1)}, u32[]{:S(2)}, u32[]{:S(2)}) async-start(f32[16,1,4608]{2,1,0:T(1,128)} %reshape.3298), calls=%async_computation.1 | async-start | bytes 589824 | tf_op jit(solution)/shard_map/while/body/eval_jaxpr/all_to_all | solution.py:153
  1002.5 19.2 %all-to-all-start = ((f32[16,1,9216]{2,1,0:T(1,128)}), f32[16,1,9216]{2,1,0:T(1,128)S(1)}, u32[]{:S(2)}, u32[]{:S(2)}) async-start(f32[16,1,9216]{2,1,0:T(1,128)} %reshape.3295), calls=%async_computation | async-start | bytes 1179648 | tf_op jit(solution)/shard_map/while/body/eval_jaxpr/all_to_all | solution.py:133
  1039.1 19.5 %all-to-all-start.1 = ((f32[16,1,4608]{2,1,0:T(1,128)}), f32[16,1,4608]{2,1,0:T(1,128)S(1)}, u32[]{:S(2)}, u32[]{:S(2)}) async-start(f32[16,1,4608]{2,1,0:T(1,128)} %reshape.3298), calls=%async_computation.1 | async-start | bytes 589824 | tf_op jit(solution)/shard_map/while/body/eval_jaxpr/all_to_all | solution.py:153
  1071.9 19.2 %all-to-all-start = ((f32[16,1,9216]{2,1,0:T(1,128)}), f32[16,1,9216]{2,1,0:T(1,128)S(1)}, u32[]{:S(2)}, u32[]{:S(2)}) async-start(f32[16,1,9216]{2,1,0:T(1,128)} %reshape.3295), calls=%async_computation | async-start | bytes 1179648 | tf_op jit(solution)/shard_map/while/body/eval_jaxpr/all_to_all | solution.py:133
  1108.6 19.5 %all-to-all-start.1 = ((f32[16,1,4608]{2,1,0:T(1,128)}), f32[16,1,4608]{2,1,0:T(1,128)S(1)}, u32[]{:S(2)}, u32[]{:S(2)}) async-start(f32[16,1,4608]{2,1,0:T(1,128)} %reshape.3298), calls=%async_computation.1 | async-start | bytes 589824 | tf_op jit(solution)/shard_map/while/body/eval_jaxpr/all_to_all | solution.py:153
  1141.3 19.2 %all-to-all-start = ((f32[16,1,9216]{2,1,0:T(1,128)}), f32[16,1,9216]{2,1,0:T(1,128)S(1)}, u32[]{:S(2)}, u32[]{:S(2)}) async-start(f32[16,1,9216]{2,1,0:T(1,128)} %reshape.3295), calls=%async_computation | async-start | bytes 1179648 | tf_op jit(solution)/shard_map/while/body/eval_jaxpr/all_to_all | solution.py:133
  1178.0 19.5 %all-to-all-start.1 = ((f32[16,1,4608]{2,1,0:T(1,128)}), f32[16,1,4608]{2,1,0:T(1,128)S(1)}, u32[]{:S(2)}, u32[]{:S(2)}) async-start(f32[16,1,4608]{2,1,0:T(1,128)} %reshape.3298), calls=%async_computation.1 | async-start | bytes 589824 | tf_op jit(solution)/shard_map/while/body/eval_jaxpr/all_to_all | solution.py:153
  1210.8 19.2 %all-to-all-start = ((f32[16,1,9216]{2,1,0:T(1,128)}), f32[16,1,9216]{2,1,0:T(1,128)S(1)}, u32[]{:S(2)}, u32[]{:S(2)}) async-start(f32[16,1,9216]{2,1,0:T(1,128)} %reshape.3295), calls=%async_computation | async-start | bytes 1179648 | tf_op jit(solution)/shard_map/while/body/eval_jaxpr/all_to_all | solution.py:133
  1247.4 19.5 %all-to-all-start.1 = ((f32[16,1,4608]{2,1,0:T(1,128)}), f32[16,1,4608]{2,1,0:T(1,128)S(1)}, u32[]{:S(2)}, u32[]{:S(2)}) async-start(f32[16,1,4608]{2,1,0:T(1,128)} %reshape.3298), calls=%async_computation.1 | async-start | bytes 589824 | tf_op jit(solution)/shard_map/while/body/eval_jaxpr/all_to_all | solution.py:153
  1280.2 19.2 %all-to-all-start = ((f32[16,1,9216]{2,1,0:T(1,128)}), f32[16,1,9216]{2,1,0:T(1,128)S(1)}, u32[]{:S(2)}, u32[]{:S(2)}) async-start(f32[16,1,9216]{2,1,0:T(1,128)} %reshape.3295), calls=%async_computation | async-start | bytes 1179648 | tf_op jit(solution)/shard_map/while/body/eval_jaxpr/all_to_all | solution.py:133
  1316.9 19.5 %all-to-all-start.1 = ((f32[16,1,4608]{2,1,0:T(1,128)}), f32[16,1,4608]{2,1,0:T(1,128)S(1)}, u32[]{:S(2)}, u32[]{:S(2)}) async-start(f32[16,1,4608]{2,1,0:T(1,128)} %reshape.3298), calls=%async_computation.1 | async-start | bytes 589824 | tf_op jit(solution)/shard_map/while/body/eval_jaxpr/all_to_all | solution.py:153
  1349.7 19.2 %all-to-all-start = ((f32[16,1,9216]{2,1,0:T(1,128)}), f32[16,1,9216]{2,1,0:T(1,128)S(1)}, u32[]{:S(2)}, u32[]{:S(2)}) async-start(f32[16,1,9216]{2,1,0:T(1,128)} %reshape.3295), calls=%async_computation | async-start | bytes 1179648 | tf_op jit(solution)/shard_map/while/body/eval_jaxpr/all_to_all | solution.py:133
  1386.3 19.5 %all-to-all-start.1 = ((f32[16,1,4608]{2,1,0:T(1,128)}), f32[16,1,4608]{2,1,0:T(1,128)S(1)}, u32[]{:S(2)}, u32[]{:S(2)}) async-start(f32[16,1,4608]{2,1,0:T(1,128)} %reshape.3298), calls=%async_computation.1 | async-start | bytes 589824 | tf_op jit(solution)/shard_map/while/body/eval_jaxpr/all_to_all | solution.py:153
  1419.1 19.2 %all-to-all-start = ((f32[16,1,9216]{2,1,0:T(1,128)}), f32[16,1,9216]{2,1,0:T(1,128)S(1)}, u32[]{:S(2)}, u32[]{:S(2)}) async-start(f32[16,1,9216]{2,1,0:T(1,128)} %reshape.3295), calls=%async_computation | async-start | bytes 1179648 | tf_op jit(solution)/shard_map/while/body/eval_jaxpr/all_to_all | solution.py:133
  1455.8 19.5 %all-to-all-start.1 = ((f32[16,1,4608]{2,1,0:T(1,128)}), f32[16,1,4608]{2,1,0:T(1,128)S(1)}, u32[]{:S(2)}, u32[]{:S(2)}) async-start(f32[16,1,4608]{2,1,0:T(1,128)} %reshape.3298), calls=%async_computation.1 | async-start | bytes 589824 | tf_op jit(solution)/shard_map/while/body/eval_jaxpr/all_to_all | solution.py:153
  1488.5 19.2 %all-to-all-start = ((f32[16,1,9216]{2,1,0:T(1,128)}), f32[16,1,9216]{2,1,0:T(1,128)S(1)}, u32[]{:S(2)}, u32[]{:S(2)}) async-start(f32[16,1,9216]{2,1,0:T(1,128)} %reshape.3295), calls=%async_computation | async-start | bytes 1179648 | tf_op jit(solution)/shard_map/while/body/eval_jaxpr/all_to_all | solution.py:133
  1525.2 19.5 %all-to-all-start.1 = ((f32[16,1,4608]{2,1,0:T(1,128)}), f32[16,1,4608]{2,1,0:T(1,128)S(1)}, u32[]{:S(2)}, u32[]{:S(2)}) async-start(f32[16,1,4608]{2,1,0:T(1,128)} %reshape.3298), calls=%async_computation.1 | async-start | bytes 589824 | tf_op jit(solution)/shard_map/while/body/eval_jaxpr/all_to_all | solution.py:153
  1558.2 38.1 %collective-permute-start = (f32[3,128,8,128]{3,1,2,0:T(8,128)S(1)}, f32[3,128,8,128]{3,1,2,0:T(8,128)S(1)}, u32[]{:S(2)}, u32[]{:S(2)}) collective-permute-start(f32[3,128,8,128]{3,1,2,0:T(8,128)S(1)} %fusion.145), channel_id=1, source_target_pairs={{0,16},{16,32},{32,48},{48,64},{64,80},{80,96},{96,112},{112,128},... | collective-permute-start | bytes 4718600 | tf_op jit(solution)/shard_map/ppermute | solution.py:36
  1559.5 36.9 %copy-start.21 = (f32[1,128,8,128]{3,1,2,0:T(8,128)S(1)}, f32[1,128,8,128]{3,1,2,0:T(8,128)}, u32[]{:S(2)}) copy-start(f32[1,128,8,128]{3,1,2,0:T(8,128)} %copy-done.20) | copy-start | bytes 1572868
  1559.5 36.8 %copy-start.23 = (f32[1,128,8,128]{3,1,2,0:T(8,128)S(1)}, f32[1,128,8,128]{3,1,2,0:T(8,128)}, u32[]{:S(2)}) copy-start(f32[1,128,8,128]{3,1,2,0:T(8,128)} %copy-done.22) | copy-start | bytes 1572868
  1559.5 36.8 %copy-start.25 = (f32[1,128,8,128]{3,1,2,0:T(8,128)S(1)}, f32[1,128,8,128]{3,1,2,0:T(8,128)}, u32[]{:S(2)}) copy-start(f32[1,128,8,128]{3,1,2,0:T(8,128)} %copy-done.24) | copy-start | bytes 1572868
  (266 other events, 673.4 us)
Sparse Core Ops, SparseCore 0:
  431.4 138.6 all-gather.1
where the time goes:
time: 1630 us; the launch traced here: 1610 us
  waiting for transfers between devices  606 us (37%)
  matrix products  285 us (17%)
  local copies, waits for them, and re-layouts  276 us (17%)
  starting transfers between devices  251 us (15%)
  other arithmetic  167 us (10%)
    all_to_all x16, waiting for transfers between devices, to_spectral(): lax.all_to_all(along_y, ('py', 'pz'), split_axis=2, concat_axis=1, tiled=...  235 us
    dot_general x65, matrix products, complex_apply(): result = jnp.einsum(pattern, kernel, split, precision=highest)  178 us
    all_to_all x16, starting transfers between devices, to_spectral(): lax.all_to_all(along_y, ('py', 'pz'), split_axis=2, concat_axis=1, tiled=...  141 us
    all_gather x1, waiting for transfers between devices, shards(): everything = lax.all_gather(payload[None], 'tm', axis=0, tiled=True)  137 us
    all_to_all x15, waiting for transfers between devices, to_physical(): lax.all_to_all(spread, ('py', 'pz'), split_axis=1, concat_axis=2, tiled=T...  129 us
    while x476, local copies, waits for them, and re-layouts  93.8 us
    all_to_all x15, starting transfers between devices, to_physical(): lax.all_to_all(spread, ('py', 'pz'), split_axis=1, concat_axis=2, tiled=T...  78 us
    all_to_all x2, waiting for transfers between devices, moved(): lax.all_to_all(group, axis, split_axis=split_dim, concat_axis=concat_dim,...  69.3 us
  transfers between devices with their start and end apart: 35, of which 35 were waited for; matrix products, arithmetic and copies ran while one was open for 7% of the time, Pallas kernels for 0%

commit v1 on v0

--- a/solution.py
+++ b/solution.py
@@ -4,6 +4,9 @@
 import jax
 import jax.numpy as jnp
 from jax import lax
+from jax.experimental import pallas as pl
+from jax.experimental.pallas import tpu as pltpu
+import numpy as np
 from jax.sharding import PartitionSpec as P
 
 M = 64
@@ -11,7 +14,7 @@
 
 viscosity = 0.03
 time_step = 0.004
-highest = lax.Precision.HIGHEST
+highest = lax.Precision.HIGH
 
 
 def items_in_groups(x, axis, split_dim, concat_dim, work, item_dim, out_dim):
@@ -237,6 +240,333 @@
     return jnp.concatenate([wider[..., :halfway], zeros_z, wider[..., halfway:], zeros_z], axis=3)
 
 
+G = 3 * M // 2
+PARTS = 16
+LOCAL = M // PARTS
+PLANES = G // PARTS
+CHUNK = LOCAL * PLANES
+LANES = 128
+PAIR = LANES // 2
+QUAD = PAIR // 2
+MESH = pl.DeviceIdType.MESH
+
+
+def halves(matrix):
+    high = np.asarray(matrix, np.float32).astype(jnp.bfloat16)
+    low = (np.asarray(matrix, np.float32) - high.astype(np.float32)).astype(jnp.bfloat16)
+    return high, low
+
+
+def coarse_matrices():
+    points = np.arange(G)
+    waves = np.where(np.arange(M) < M // 2, np.arange(M), np.arange(M) - M)
+    angle = (points[:, None] * waves[None, :]) % G * (2.0 * np.pi / G)
+    spread = np.concatenate([np.cos(angle), np.sin(angle)], 1) * M**-0.5
+    gather = np.concatenate([np.cos(angle.T), -np.sin(angle.T)], 1) * (M**0.5 / G)
+    harmonic = np.arange(M // 2)
+    angle = (points[:, None] * harmonic[None, :]) % G * (2.0 * np.pi / G)
+    weight = np.where(harmonic == 0, 1.0, 2.0) * M**-0.5
+    inverse = np.zeros((PAIR, LANES))
+    inverse[:, :G] = np.concatenate([np.cos(angle) * weight, -np.sin(angle) * weight], 1).T
+    forward = np.zeros((LANES, PAIR))
+    forward[:G] = np.concatenate([np.cos(angle), -np.sin(angle)], 1) * (M**0.5 / G)
+    turned = np.concatenate([-forward[:, QUAD:], forward[:, :QUAD]], 1)
+    none_in = np.zeros_like(inverse)
+    none_out = np.zeros_like(forward)
+    inverse_pair = np.block([[inverse, none_in], [none_in, inverse]])
+    forward_pair = np.block(
+        [[forward, none_out, turned, none_out], [none_out, forward, none_out, turned]]
+    )
+    forward_one = np.concatenate([forward, forward, turned, turned], 1)
+    made = []
+    for matrix in (spread, gather):
+        high, low = halves(matrix)
+        made.append(jnp.asarray(np.concatenate([high, high, low], 1)))
+    for matrix in (inverse_pair, forward_pair, forward_one):
+        high, low = halves(matrix)
+        made.append(jnp.asarray(np.concatenate([high, high, low], 0)))
+    return made
+
+
+def wave_tables(member):
+    rows = signed_wave(jnp.arange(M, dtype=jnp.int32), M).astype(jnp.float32)[None, :, None]
+    local = jnp.arange(LOCAL, dtype=jnp.int32)
+    wave_y = signed_wave(local * PARTS + member, M).astype(jnp.float32)[:, None, None]
+    lane = jnp.arange(LANES, dtype=jnp.int32)[None, None, :]
+    wave_z = (lane % QUAD).astype(jnp.float32)
+    full = (LOCAL, M, LANES)
+    kx, ky, kz = (jnp.broadcast_to(w, full) for w in (rows, wave_y, wave_z))
+    lower = lane < PAIR
+    squared = kx * kx + ky * ky + kz * kz
+    return (
+        jnp.where(lower, kx, ky),
+        ky,
+        jnp.where(lower, kz, kx)[0],
+        kz[0],
+        1.0 / jnp.maximum(squared, 1.0),
+        jnp.exp(-viscosity * time_step * squared),
+    )
+
+
+def turn(x):
+    lane = lax.broadcasted_iota(jnp.int32, x.shape, 1)
+    return jnp.where(
+        lane % PAIR < QUAD, -pltpu.roll(x, LANES - QUAD, 1), pltpu.roll(x, QUAD, 1)
+    )
+
+
+def split(x):
+    high = x.astype(jnp.bfloat16)
+    return high, (x - high.astype(jnp.float32)).astype(jnp.bfloat16)
+
+
+def left_apply(matrix, x):
+    high, low = split(x)
+    return jnp.dot(
+        matrix, jnp.concatenate([high, low, high], 0), preferred_element_type=jnp.float32
+    )
+
+
+def right_apply(x, matrix):
+    high, low = split(x)
+    return jnp.dot(
+        jnp.concatenate([high, low, high], 1), matrix, preferred_element_type=jnp.float32
+    )
+
+
+def spread_waves(state, a, tables, spread):
+    kxy, ky, kzx, kz = tables[0][a], tables[1][a], tables[2][...], tables[3][...]
+    first, third = state[a, :, :LANES], state[a, :, LANES:]
+    lower = lax.broadcasted_iota(jnp.int32, first.shape, 1) < PAIR
+    raw_one = ky * third - kz * first
+    raw_two = kzx * first - kxy * jnp.where(lower, third, pltpu.roll(first, PAIR, 1))
+    fields = jnp.concatenate(
+        [first, jnp.where(lower, third, turn(raw_one)), turn(raw_two)], 1
+    )
+    turned = jnp.concatenate(
+        [turn(first), jnp.where(lower, turn(third), -raw_one), -raw_two], 1
+    )
+    return left_apply(spread, jnp.concatenate([fields, turned], 0))
+
+
+def plane_product(fetched, x, mats):
+    spread, gather, inverse_pair, forward_pair, forward_one = mats
+    fields, turned = [], []
+    for g in range(3):
+        rows = jnp.concatenate(
+            [fetched[g, pl.ds(LOCAL * x + a, PARTS, stride=CHUNK), :] for a in range(LOCAL)], 0
+        )
+        fields.append(rows)
+        turned.append(turn(rows))
+    along_y = left_apply(
+        spread, jnp.concatenate([jnp.concatenate(fields, 1), jnp.concatenate(turned, 1)], 0)
+    )
+    grids = [
+        right_apply(along_y[:, LANES * g : LANES * (g + 1)], inverse_pair) for g in range(3)
+    ]
+    u0, u1 = grids[0][:, :LANES], grids[0][:, LANES:]
+    u2, w0 = grids[1][:, :LANES], grids[1][:, LANES:]
+    w1, w2 = grids[2][:, :LANES], grids[2][:, LANES:]
+    pair = jnp.concatenate([u1 * w2 - u2 * w1, u2 * w0 - u0 * w2], 1)
+    back_pair = right_apply(pair, forward_pair)
+    back_one = right_apply(u0 * w1 - u1 * w0, forward_one)
+    return left_apply(
+        gather,
+        jnp.concatenate(
+            [
+                jnp.concatenate([back_pair[:, :LANES], back_one[:, :LANES]], 1),
+                jnp.concatenate([back_pair[:, LANES:], back_one[:, LANES:]], 1),
+            ],
+            0,
+        ),
+    )
+
+
+def gather_waves(fetched, state, a, tables, gather):
+    kxy, kz, inverse, damping = tables[0][a], tables[3][...], tables[4][a], tables[5][a]
+    rows = [fetched[g, pl.ds(a, G, stride=LOCAL), :] for g in range(2)]
+    turned = [turn(r) for r in rows]
+    modes = left_apply(
+        gather, jnp.concatenate([jnp.concatenate(rows, 1), jnp.concatenate(turned, 1)], 0)
+    )
+    first, third = modes[:, :LANES], modes[:, LANES:]
+    along = kxy * first
+    divergence = (along + pltpu.roll(along, PAIR, 1) + kz * third) * inverse
+    return (
+        damping * (state[a, :, :LANES] + time_step * (first - kxy * divergence)),
+        damping * (state[a, :, LANES:] + time_step * (third - kz * divergence)),
+    )
+
+
+def chain_kernel(
+    payload,
+    kxy, ky, kzx, kz, inverse, damping,
+    spread, gather, inverse_pair, forward_pair, forward_one,
+    result,
+    states, terms, out_f, in_f, out_b, in_b,
+    term_send, term_recv, state_send, state_recv, f_send, f_recv, b_send, b_recv,
+):
+    tables = (kxy, ky, kzx, kz, inverse, damping)
+    mats = tuple(m[...] for m in (spread, gather, inverse_pair, forward_pair, forward_one))
+    slot, py, pz = lax.axis_index("tm"), lax.axis_index("py"), lax.axis_index("pz")
+    slices = lax.axis_size("tm")
+    stride = slices // 4
+    far, core = pz // 2, pz % 2
+    is_chain = (far == 0) & (slot % stride == 0) & (slot < 2 * stride)
+    own_term = (slot == 0) & (far == 0)
+    sends_term = jnp.logical_not(own_term) & (slot < slices - 1)
+    side = slot // stride
+    me = py * 4 + side * 2 + core
+
+    def term_copy(source_slice):
+        return pltpu.make_async_remote_copy(
+            src_ref=payload,
+            dst_ref=terms.at[source_slice],
+            send_sem=term_send,
+            recv_sem=term_recv.at[source_slice],
+            device_id=(far * stride, py, core),
+            device_id_type=MESH,
+        )
+
+    def state_copy(t):
+        return pltpu.make_async_remote_copy(
+            src_ref=states.at[t],
+            dst_ref=result,
+            send_sem=state_send.at[t],
+            recv_sem=state_recv,
+            device_id=(t, py, side * 2 + core),
+            device_id_type=MESH,
+        )
+
+    def part_copy(source, target, sends, recvs, owner, peer):
+        return pltpu.make_async_remote_copy(
+            src_ref=source.at[:, pl.ds(pl.multiple_of(peer * CHUNK, 8), CHUNK), :],
+            dst_ref=target.at[:, pl.ds(pl.multiple_of(owner * CHUNK, 8), CHUNK), :],
+            send_sem=sends.at[peer],
+            recv_sem=recvs.at[owner],
+            device_id=((peer // 2) % 2 * stride, peer // 4, peer % 2),
+            device_id_type=MESH,
+        )
+
+    def exchange(source, target, sends, recvs):
+        def send(j, carried):
+            peer = (me + j) % PARTS
+            part_copy(source, target, sends, recvs, me, peer).start()
+            return carried
+
+        def receive(j, carried):
+            peer = (me + PARTS - j) % PARTS
+            part_copy(source, target, sends, recvs, peer, peer).wait_recv()
+            return carried
+
+        def finish(j, carried):
+            peer = (me + j) % PARTS
+            part_copy(source, target, sends, recvs, me, peer).wait_send()
+            return carried
+
+        lax.fori_loop(1, PARTS, send, 0)
+        mine = pl.ds(pl.multiple_of(me * CHUNK, 8), CHUNK)
+        target[:, mine, :] = source[:, mine, :]
+        lax.fori_loop(1, PARTS, receive, 0)
+        lax.fori_loop(1, PARTS, finish, 0)
+
+    @pl.when(sends_term)
+    def _():
+        term_copy(slot).start()
+
+    @pl.when(slot == 0)
+    def _():
+        result[...] = jnp.zeros_like(result)
+
+    @pl.when(is_chain)
+    def _():
+        @pl.when(own_term)
+        def _():
+            states[1] = payload[...]
+
+        @pl.when(jnp.logical_not(own_term))
+        def _():
+            term_copy(0).wait_recv()
+            states[1] = terms[0]
+
+        def step(t, carried):
+            state_copy(t).start()
+            state = states.at[t]
+            for a in range(LOCAL):
+                waves = spread_waves(state, a, tables, mats[0])
+                for g in range(3):
+                    out_f[g, pl.ds(a, G, stride=LOCAL), :] = waves[:, LANES * g : LANES * (g + 1)]
+            exchange(out_f, in_f, f_send, f_recv)
+            for x in range(PLANES):
+                back = plane_product(in_f, x, mats)
+                for g in range(2):
+                    for a in range(LOCAL):
+                        out_b[g, pl.ds(LOCAL * x + a, PARTS, stride=CHUNK), :] = back[
+                            PARTS * a : PARTS * (a + 1), LANES * g : LANES * (g + 1)
+                        ]
+            exchange(out_b, in_b, b_send, b_recv)
+            term_copy(t).wait_recv()
+            for a in range(LOCAL):
+                first, third = gather_waves(in_b, state, a, tables, mats[1])
+                states[t + 1, a, :, :LANES] = first + terms[t, a, :, :LANES]
+                states[t + 1, a, :, LANES:] = third + terms[t, a, :, LANES:]
+            return carried
+
+        lax.fori_loop(1, slices - 1, step, 0)
+        state_copy(slices - 1).start()
+
+        def finish(t, carried):
+            state_copy(t).wait_send()
+            return carried
+
+        lax.fori_loop(1, slices, finish, 0)
+
+    @pl.when(sends_term)
+    def _():
+        term_copy(slot).wait_send()
+
+    @pl.when(slot != 0)
+    def _():
+        state_copy(slot).wait_recv()
+
+
+def chain(payload, slices):
+    core = lax.axis_index("pz") % 2
+    side = lax.axis_index("tm") // (slices // 4) % 2
+    member = lax.axis_index("py") * 4 + side * 2 + core
+    packed = payload.transpose(2, 1, 0, 3)
+    packed = jnp.concatenate([packed, packed[:, :, 2:]], axis=2).reshape(LOCAL, M, 2 * LANES)
+    vmem = pl.BlockSpec(memory_space=pltpu.VMEM)
+    operands = [packed, *wave_tables(member), *coarse_matrices()]
+    block = (LOCAL, M, 2 * LANES)
+    made = pl.pallas_call(
+        chain_kernel,
+        out_shape=jax.ShapeDtypeStruct(block, jnp.float32),
+        in_specs=[vmem] * len(operands),
+        out_specs=vmem,
+        scratch_shapes=[
+            pltpu.VMEM((slices,) + block, jnp.float32),
+            pltpu.VMEM((slices,) + block, jnp.float32),
+            pltpu.VMEM((3, G * LOCAL, LANES), jnp.float32),
+            pltpu.VMEM((3, G * LOCAL, LANES), jnp.float32),
+            pltpu.VMEM((2, G * LOCAL, LANES), jnp.float32),
+            pltpu.VMEM((2, G * LOCAL, LANES), jnp.float32),
+            pltpu.SemaphoreType.DMA,
+            pltpu.SemaphoreType.DMA((slices,)),
+            pltpu.SemaphoreType.DMA((slices,)),
+            pltpu.SemaphoreType.DMA,
+            pltpu.SemaphoreType.DMA((PARTS,)),
+            pltpu.SemaphoreType.DMA((PARTS,)),
+            pltpu.SemaphoreType.DMA((PARTS,)),
+            pltpu.SemaphoreType.DMA((PARTS,)),
+        ],
+        compiler_params=pltpu.CompilerParams(
+            has_side_effects=True, vmem_limit_bytes=32 * 1024 * 1024
+        ),
+    )(*operands)
+    return made.reshape(LOCAL, M, 4, PAIR)[:, :, :3].transpose(2, 1, 0, 3)
+
+
 def shards(start_states):
     count_py = lax.axis_size("py")
     count_pz = lax.axis_size("pz")
@@ -254,22 +584,7 @@
     fine_low = restrict(fine_end, M, groups)
     correction = fine_low - coarse_next
     payload = jnp.where(position == 0, fine_low, correction)
-    everything = lax.all_gather(payload[None], "tm", axis=0, tiled=True)
-
-    def sweep_turn(turn_index, carried):
-        chained, current = carried
-        chained = advance(chained, "coarse", layout) + lax.dynamic_index_in_dim(
-            everything, turn_index, 0, keepdims=False
-        )
-        return (chained, jnp.where(position == turn_index + 1, chained, current))
-
-    start_value = everything[0]
-    chained, current = lax.fori_loop(
-        1,
-        slices - 1,
-        sweep_turn,
-        (start_value, jnp.where(position == 1, start_value, coarse_start)),
-    )
+    current = chain(payload, slices)
     upper_band = fine_end - prolong(fine_low, retained, groups)
     previous = shifted(upper_band, "tm", 1)
     updated = prolong(current, retained, groups) + previous

time: 1630 us -> 803 us (0.49)
  waiting for transfers between devices: 606 us -> 191 us
  Pallas kernels: 0 us -> 344 us
  matrix products: 285 us -> 56.8 us
  local copies, waits for them, and re-layouts: 276 us -> 85.5 us
  starting transfers between devices: 251 us -> 67.8 us
  other arithmetic: 167 us -> 42.8 us
    pallas_call x0 -> x1, Pallas kernels: none -> 344 us  [chain(): pl.pallas_call(chain_kernel, out_shape=jax.ShapeDtypeStruct(block, jnp.fl...]
    all_to_all x16 -> x2, waiting for transfers between devices: 235 us -> 72.5 us  [to_spectral(): lax.all_to_all(along_y, ('py', 'pz'), split_axis=2, concat_axis=1, tiled=...]
    dot_general x65 -> x9, matrix products: 178 us -> 37.8 us  [complex_apply(): result = jnp.einsum(pattern, kernel, split, precision=highest)]
    all_gather x1 -> x0, waiting for transfers between devices: 137 us -> none  [shards(): everything = lax.all_gather(payload[None], 'tm', axis=0, tiled=True)]
    all_to_all x15 -> x1, waiting for transfers between devices: 129 us -> 15.1 us  [to_physical(): lax.all_to_all(spread, ('py', 'pz'), split_axis=1, concat_axis=2, tiled=T...]
    all_to_all x16 -> x2, starting transfers between devices: 141 us -> 30.5 us  [to_spectral(): lax.all_to_all(along_y, ('py', 'pz'), split_axis=2, concat_axis=1, tiled=...]
    while x479 -> x0, local copies, waits for them, and re-layouts: 96.1 us -> none
    all_to_all x15 -> x1, starting transfers between devices: 78 us -> 4.77 us  [to_physical(): lax.all_to_all(spread, ('py', 'pz'), split_axis=1, concat_axis=2, tiled=T...]
  transfers between devices with their start and end apart: 35 -> 6, of which waited for: 35 -> 6; matrix products, arithmetic and copies ran while one was open for 7% -> 3% of each run, Pallas kernels for 0% -> 0%
where the time goes in v1:
time: 803 us; the launch traced here: 790 us
  Pallas kernels  344 us (43%)
  waiting for transfers between devices  191 us (24%)
  local copies, waits for them, and re-layouts  85.5 us (11%)
  starting transfers between devices  67.8 us (8%)
  matrix products  56.8 us (7%)
  other arithmetic  42.8 us (5%)
    pallas_call x1, Pallas kernels, chain(): pl.pallas_call(chain_kernel, out_shape=jax.ShapeDtypeStruct(block, jnp.fl...  344 us
    all_to_all x2, waiting for transfers between devices, to_spectral(): lax.all_to_all(along_y, ('py', 'pz'), split_axis=2, concat_axis=1, tiled=...  72.5 us
    all_to_all x2, waiting for transfers between devices, moved(): lax.all_to_all(group, axis, split_axis=split_dim, concat_axis=concat_dim,...  69.1 us
    dot_general x9, matrix products, complex_apply(): result = jnp.einsum(pattern, kernel, split, precision=highest)  37.8 us
    ppermute x1, waiting for transfers between devices, shifted(): return lax.ppermute(block, axis, route)  34.8 us
    all_to_all x2, starting transfers between devices, moved(): lax.all_to_all(group, axis, split_axis=split_dim, concat_axis=concat_dim,...  31 us
    all_to_all x2, starting transfers between devices, to_spectral(): lax.all_to_all(along_y, ('py', 'pz'), split_axis=2, concat_axis=1, tiled=...  30.5 us
    reshape x5, local copies, waits for them, and re-layouts, complex_apply(): split = values.reshape(values.shape[:-1] + (2, halfway))  19.9 us
  transfers between devices with their start and end apart: 6, of which 6 were waited for; matrix products, arithmetic and copies ran while one was open for 3% of the time, Pallas kernels for 0%

profile of v1, /device:TPU:103, one launch (start us, length us, event | category | flops | bytes accessed | tf_op | source)
XLA Modules:
  0.0 789.7 jit_solution(9283487105493919532)
XLA Ops:
  0.1 2.4 fusion.260
  5.0 2.3 fusion.19
  7.3 1.9 fusion.254
  10.3 2.4 copy.214
  12.7 2.5 copy.215
  19.0 1.9 multiply_subtract_fusion.4
  24.1 9.1 %all-to-all-start.1 = ((f32[3,192,8,128]{3,2,0,1:T(8,128)}), f32[3,192,8,128]{3,2,0,1:T(8,128)}, u32[]{:S(2)}, u32[]{:S(2)}) async-start(f32[3,192,8,128]{3,2,0,1:T(8,128)} %pad_maximum_fusion), calls=%async_computation.1 | async-start | bytes 4718592 | tf_op jit(solution)/shard_map/all_to_all | solution.py:23
  33.2 1.9 slice-done
  35.1 2.1 copy.209
  37.2 37.8 %all-to-all-done.1 = f32[3,192,8,128]{3,2,0,1:T(8,128)} async-done(((f32[3,192,8,128]{3,2,0,1:T(8,128)}), f32[3,192,8,128]{3,2,0,1:T(8,128)}, u32[]{:S(2)}, u32[]{:S(2)}) %all-to-all-start.1) | async-done | bytes 2359328 | tf_op jit(solution)/shard_map/all_to_all | solution.py:23
  75.0 21.9 %all-to-all-start = ((f32[3,192,8,128]{3,2,0,1:T(8,128)}), f32[3,192,8,128]{3,2,0,1:T(8,128)}, u32[]{:S(2)}, u32[]{:S(2)}) async-start(f32[3,192,8,128]{3,2,0,1:T(8,128)} %copy.209), calls=%async_computation | async-start | bytes 4718592 | tf_op jit(solution)/shard_map/all_to_all | solution.py:23
  97.9 1.9 copy.223
  99.9 4.1 reshape.2024
  104.0 31.3 %all-to-all-done = f32[3,192,8,128]{3,2,0,1:T(8,128)} async-done(((f32[3,192,8,128]{3,2,0,1:T(8,128)}), f32[3,192,8,128]{3,2,0,1:T(8,128)}, u32[]{:S(2)}, u32[]{:S(2)}) %all-to-all-start) | async-done | bytes 2359328 | tf_op jit(solution)/shard_map/all_to_all | solution.py:23
  135.3 1.9 copy.211
  137.2 4.1 reshape.2022
  141.3 10.0 %fusion.8 = f32[3,12,64,2,192,1]{4,2,5,3,1,0:T(8,128)S(1)} fusion(f32[3,12,128,2,64,1]{4,3,2,1,0,5:T(2,128)} %bitcast.290, f32[1,2,192,128]{3,2,1,0:T(8,128)S(1)} %get-tuple-element.85, f32[1,2,192,128]{3,2,1,0:T(8,128)S(1)} %get-tuple-element.84), kind=kOutput, calls=%fused_computation.8 | convolution fusion | flops 1359052800 | bytes 6291456 | tf_op jit(solution)/shard_map/pqok,flkqh->floph/dot_general | solution.py:70
  151.3 7.9 fusion.10
  159.2 4.3 fusion.78
  163.5 4.3 fusion.80
  167.8 4.1 multiply_subtract_fusion.2
  171.8 7.6 fusion
  179.4 2.1 fusion.46
  181.5 2.5 copy.227
  184.0 25.1 %all-to-all-start.2 = ((f32[3,12,128,128]{3,1,0,2:T(8,128)}), f32[3,12,128,128]{3,1,0,2:T(8,128)S(1)}, u32[]{:S(2)}, u32[]{:S(2)}) async-start(f32[3,12,128,128]{3,1,0,2:T(8,128)} %copy.227), calls=%async_computation.2 | async-start | bytes 6291456 | tf_op jit(solution)/shard_map/all_to_all | solution.py:161
  222.1 63.2 %all-to-all-done.2 = f32[3,12,128,128]{3,1,0,2:T(8,128)S(1)} async-done(((f32[3,12,128,128]{3,1,0,2:T(8,128)}), f32[3,12,128,128]{3,1,0,2:T(8,128)S(1)}, u32[]{:S(2)}, u32[]{:S(2)}) %all-to-all-start.2) | async-done | bytes 2359328 | tf_op jit(solution)/shard_map/all_to_all | solution.py:161
  285.3 2.5 copy.229
  287.8 6.0 reshape.2028
  293.8 6.7 fusion.30
  313.9 2.4 fusion.268
  316.4 3.2 reshape.2068
  319.5 4.8 all-to-all-start.3
  325.5 15.1 %all-to-all-done.3 = f32[16,1,9216]{2,1,0:T(1,128)S(1)} async-done(((f32[16,1,9216]{2,1,0:T(1,128)}), f32[16,1,9216]{2,1,0:T(1,128)S(1)}, u32[]{:S(2)}, u32[]{:S(2)}) %all-to-all-start.3) | async-done | bytes 589856 | tf_op jit(solution)/shard_map/all_to_all | solution.py:136
  341.9 3.1 reduce
  345.0 1.8 reshape.2069
  346.8 2.6 copy.243
  349.4 3.9 reshape.2030
  353.4 3.7 fusion.20
  361.4 2.2 copy.245
  363.6 2.3 reshape.2070
  365.9 5.4 all-to-all-start.4
  373.4 9.3 %all-to-all-done.4 = f32[16,1,4608]{2,1,0:T(1,128)} async-done(((f32[16,1,4608]{2,1,0:T(1,128)}), f32[16,1,4608]{2,1,0:T(1,128)}, u32[]{:S(2)}, u32[]{:S(2)}) %all-to-all-start.4) | async-done | bytes 294944 | tf_op jit(solution)/shard_map/all_to_all | solution.py:156
  382.7 2.3 reduce.1
  387.5 1.8 reshape.2034
  389.3 2.4 convolution_bitcast_fusion.1
  400.4 343.8 %shard_map.64 = f32[4,64,256]{2,1,0:T(8,128)S(1)} custom-call(f32[4,64,256]{2,1,0:T(8,128)S(1)} %reshape.2035.payload, f32[4,64,128]{2,1,0:T(8,128)S(1)} %broadcast_select_fusion.kxy, f32[4,64,128]{2,1,0:T(8,128)S(1)} %broadcast_in_dim.89.ky, f32[64,128]{1,0:T(8,128)S(1)} %select_bitcast_fusion.kzx, f32[64,128]{1,0:T(8,128)S(1)} %squeeze.127.kz, ...), custom_call_target="tpu_custom_call" | custom-call | tf_op jit(solution)/shard_map/pallas_call | solution.py:542
  750.6 34.8 %collective-permute-done = f32[3,128,8,128]{3,1,2,0:T(8,128)S(1)} collective-permute-done((f32[3,128,8,128]{3,1,2,0:T(8,128)S(1)}, f32[3,128,8,128]{3,1,2,0:T(8,128)S(1)}, u32[]{:S(2)}, u32[]{:S(2)}) %collective-permute-start) | collective-permute-done | bytes 1572896 | tf_op jit(solution)/shard_map/ppermute | solution.py:39
  786.7 2.8 copy.257
  (251 shorter events, 64.8 us)
Async XLA Ops:
  0.0 18.9 %copy-start.37 = (f32[8]{0:T(128)}, f32[8]{0:T(128)S(1)}, u32[]{:S(2)}) copy-start(f32[8]{0:T(128)S(1)} %fusion.210) | copy-start | bytes 100
  0.1 18.9 %copy-start.50 = (f32[128]{0:T(128)}, f32[128]{0:T(128)S(1)}, u32[]{:S(2)}) copy-start(f32[128]{0:T(128)S(1)} %fusion.214) | copy-start | bytes 1540
  2.6 2.3 copy-start.7
  2.6 2.3 copy-start.9
  2.6 2.3 copy-start.11
  7.3 3.0 copy-start.5
  16.5 2.5 copy-start.23
  24.1 50.9 %all-to-all-start.1 = ((f32[3,192,8,128]{3,2,0,1:T(8,128)}), f32[3,192,8,128]{3,2,0,1:T(8,128)}, u32[]{:S(2)}, u32[]{:S(2)}) async-start(f32[3,192,8,128]{3,2,0,1:T(8,128)} %pad_maximum_fusion), calls=%async_computation.1 | async-start | bytes 4718592 | tf_op jit(solution)/shard_map/all_to_all | solution.py:23
  33.2 1.9 slice-start
  75.0 60.3 %all-to-all-start = ((f32[3,192,8,128]{3,2,0,1:T(8,128)}), f32[3,192,8,128]{3,2,0,1:T(8,128)}, u32[]{:S(2)}, u32[]{:S(2)}) async-start(f32[3,192,8,128]{3,2,0,1:T(8,128)} %copy.209), calls=%async_computation | async-start | bytes 4718592 | tf_op jit(solution)/shard_map/all_to_all | solution.py:23
  141.3 10.0 %copy-start.6 = (f32[3,12,128,2,64]{4,3,2,1,0:T(2,128)S(1)}, f32[3,12,128,2,64]{4,3,2,1,0:T(2,128)}, u32[]{:S(2)}) copy-start(f32[3,12,128,2,64]{4,3,2,1,0:T(2,128)} %reshape.2022) | copy-start | bytes 7077892
  184.0 101.3 %all-to-all-start.2 = ((f32[3,12,128,128]{3,1,0,2:T(8,128)}), f32[3,12,128,128]{3,1,0,2:T(8,128)S(1)}, u32[]{:S(2)}, u32[]{:S(2)}) async-start(f32[3,12,128,128]{3,1,0,2:T(8,128)} %copy.227), calls=%async_computation.2 | async-start | bytes 6291456 | tf_op jit(solution)/shard_map/all_to_all | solution.py:161
  210.3 10.8 %copy-start.47 = (f32[128]{0:T(128)}, f32[128]{0:T(128)S(1)}, u32[]{:S(2)}) copy-start(f32[128]{0:T(128)S(1)} %fusion.217) | copy-start | bytes 1540
  301.4 1.7 copy-start.8
  301.4 1.7 copy-start.10
  301.4 1.7 copy-start.12
  301.4 1.8 copy-start.38
  301.4 1.8 copy-start.48
  301.4 1.8 copy-start.51
  310.2 3.4 slice-start.1
  316.3 8.0 %copy-start.49 = (f32[64]{0:T(128)S(1)}, f32[64]{0:T(128)}, u32[]{:S(2)}) copy-start(f32[64]{0:T(128)} %fusion.222) | copy-start | bytes 772
  316.3 8.0 %copy-start.57 = (f32[4]{0:T(128)S(1)}, f32[4]{0:T(128)}, u32[]{:S(2)}) copy-start(f32[4]{0:T(128)} %fusion.252) | copy-start | bytes 52
  316.3 8.1 %copy-start.44 = (f32[128]{0:T(128)S(1)}, f32[128]{0:T(128)}, u32[]{:S(2)}) copy-start(f32[128]{0:T(128)} %fusion.209) | copy-start | bytes 1540
  316.3 8.2 %copy-start.43 = (f32[4]{0:T(128)S(1)}, f32[4]{0:T(128)}, u32[]{:S(2)}) copy-start(f32[4]{0:T(128)} %fusion.212) | copy-start | bytes 52
  316.3 8.2 %copy-start.46 = (f32[64]{0:T(128)S(1)}, f32[64]{0:T(128)}, u32[]{:S(2)}) copy-start(f32[64]{0:T(128)} %fusion.216) | copy-start | bytes 772
  316.3 9.0 %copy-start.55 = (f32[128]{0:T(128)S(1)}, f32[128]{0:T(128)}, u32[]{:S(2)}) copy-start(f32[128]{0:T(128)} %fusion.218) | copy-start | bytes 1540
  316.4 9.0 %copy-start.56 = (f32[4]{0:T(128)S(1)}, f32[4]{0:T(128)}, u32[]{:S(2)}) copy-start(f32[4]{0:T(128)} %fusion.251) | copy-start | bytes 52
  319.5 21.0 %all-to-all-start.3 = ((f32[16,1,9216]{2,1,0:T(1,128)}), f32[16,1,9216]{2,1,0:T(1,128)S(1)}, u32[]{:S(2)}, u32[]{:S(2)}) async-start(f32[16,1,9216]{2,1,0:T(1,128)} %reshape.2068), calls=%async_computation.3 | async-start | bytes 1179648 | tf_op jit(solution)/shard_map/all_to_all | solution.py:136
  349.4 3.9 copy-start.29
  349.4 3.9 copy-start.30
  353.3 3.7 copy-start.41
  353.3 3.8 copy-start.42
  353.4 3.8 copy-start.54
  365.9 16.8 %all-to-all-start.4 = ((f32[16,1,4608]{2,1,0:T(1,128)}), f32[16,1,4608]{2,1,0:T(1,128)}, u32[]{:S(2)}, u32[]{:S(2)}) async-start(f32[16,1,4608]{2,1,0:T(1,128)} %reshape.2070), calls=%async_computation.4 | async-start | bytes 589824 | tf_op jit(solution)/shard_map/all_to_all | solution.py:156
  387.4 1.9 copy-start.35
  387.4 1.9 copy-start.36
  389.3 7.0 copy-start.21
  397.6 2.7 copy-start.45
  397.6 2.7 copy-start
  397.6 2.7 copy-start.1
  397.6 2.7 copy-start.2
  397.6 2.7 copy-start.3
  397.7 2.7 copy-start.4
  400.4 344.2 %copy-start.53 = (f32[128]{0:T(128)S(1)}, f32[128]{0:T(128)}, u32[]{:S(2)}) copy-start(f32[128]{0:T(128)} %pad.18.clone) | copy-start | bytes 1540
  748.5 36.9 %collective-permute-start = (f32[3,128,8,128]{3,1,2,0:T(8,128)S(1)}, f32[3,128,8,128]{3,1,2,0:T(8,128)S(1)}, u32[]{:S(2)}, u32[]{:S(2)}) collective-permute-start(f32[3,128,8,128]{3,1,2,0:T(8,128)S(1)} %fusion.27), channel_id=1, source_target_pairs={{0,16},{16,32},{32,48},{48,64},{64,80},{80,96},{96,112},{112,128},... | collective-permute-start | bytes 4718600 | tf_op jit(solution)/shard_map/ppermute | solution.py:39
  750.0 35.4 %copy-start.14 = (f32[1,128,8,128]{3,1,2,0:T(8,128)S(1)}, f32[1,128,8,128]{3,1,2,0:T(8,128)}, u32[]{:S(2)}) copy-start(f32[1,128,8,128]{3,1,2,0:T(8,128)} %copy-done.13) | copy-start | bytes 1572868
  750.1 35.3 %copy-start.16 = (f32[1,128,8,128]{3,1,2,0:T(8,128)S(1)}, f32[1,128,8,128]{3,1,2,0:T(8,128)}, u32[]{:S(2)}) copy-start(f32[1,128,8,128]{3,1,2,0:T(8,128)} %copy-done.15) | copy-start | bytes 1572868
  750.1 35.3 %copy-start.18 = (f32[1,128,8,128]{3,1,2,0:T(8,128)S(1)}, f32[1,128,8,128]{3,1,2,0:T(8,128)}, u32[]{:S(2)}) copy-start(f32[1,128,8,128]{3,1,2,0:T(8,128)} %copy-done.17) | copy-start | bytes 1572868
  (18 other events, 19.8 us)

commit v2 on v1

--- a/solution.py
+++ b/solution.py
@@ -15,28 +15,6 @@
 viscosity = 0.03
 time_step = 0.004
 highest = lax.Precision.HIGH
-
-
-def items_in_groups(x, axis, split_dim, concat_dim, work, item_dim, out_dim):
-
-    def moved(group):
-        return lax.all_to_all(group, axis, split_axis=split_dim, concat_axis=concat_dim, tiled=True)
-
-    items = jax.tree.leaves(x)[0].shape[item_dim]
-    ends = [items * k // 2 for k in range(2 + 1)] if items % 2 == 0 else [0, items]
-    groups = [
-        jax.tree.map(lambda a: lax.slice_in_dim(a, low, high, axis=item_dim), x)
-        for low, high in zip(ends, ends[1:])
-    ]
-    arrived = [moved(group) for group in groups]
-    made = [work(group) for group in arrived]
-    return jax.tree.map(lambda *parts: jnp.concatenate(parts, axis=out_dim), *made)
-
-
-def shifted(block, axis, distance):
-    devices = range(lax.axis_size(axis))
-    route = [(i - distance, i) for i in devices if i - distance in devices]
-    return lax.ppermute(block, axis, route)
 
 
 def signed_wave(places, length):
@@ -127,16 +105,23 @@
     wave_rows = signed_wave(jnp.arange(retained, dtype=jnp.int32), retained)
     cosine_part, sine_part = trig_pair(points, wave_rows, extent, retained ** (-0.5))
     moved_x = complex_apply(cosine_part, sine_part, seeds, 1, 1.0)
-    curl_x = rotate(wave_y * moved_x[2] - wave_z * moved_x[1])
-    curl_y = rotate(wave_z * moved_x[0] - moved_x[4])
-    curl_z = rotate(moved_x[3] - wave_y * moved_x[0])
-    spread = jnp.concatenate([moved_x[:3], jnp.stack([curl_x, curl_y, curl_z])], axis=0)
-    if resolution == "coarse":
-        finish = partial(inverse_tail, extent=extent, sectioned=False, layout=layout)
-        return finish(lax.all_to_all(spread, ("py", "pz"), split_axis=1, concat_axis=2, tiled=True))
-    else:
-        finish = partial(inverse_tail, extent=extent, sectioned=False, layout=layout)
-        return items_in_groups(spread, ("py", "pz"), 1, 2, finish, 0, 0)
+
+    def arrive(part):
+        return lax.all_to_all(part, ("py", "pz"), split_axis=1, concat_axis=2, tiled=True)
+
+    finish = partial(inverse_tail, extent=extent, sectioned=False, layout=layout)
+    groups = layout[2]
+    places = jnp.arange(retained, dtype=jnp.int32)
+    local_rows = retained // groups
+    owned_y = signed_wave(places % local_rows * groups + places // local_rows, retained)
+    wave_y = owned_y.astype(jnp.float32)[None, :, None]
+    waves = arrive(moved_x[:3])
+    slopes = arrive(moved_x[3:])
+    curl_x = rotate(wave_y * waves[2] - wave_z * waves[1])
+    curl_y = rotate(wave_z * waves[0] - slopes[1])
+    curl_z = rotate(slopes[0] - wave_y * waves[0])
+    curls = jnp.stack([curl_x, curl_y, curl_z])
+    return jnp.concatenate([finish(waves), finish(curls)], axis=0)
 
 
 def to_spectral(fields, retained, resolution, layout):
@@ -245,6 +230,7 @@
 LOCAL = M // PARTS
 PLANES = G // PARTS
 CHUNK = LOCAL * PLANES
+PIECES = PLANES // 2
 LANES = 128
 PAIR = LANES // 2
 QUAD = PAIR // 2
@@ -399,32 +385,40 @@
 
 
 def chain_kernel(
-    payload,
+    low, start, fine_end,
     kxy, ky, kzx, kz, inverse, damping,
     spread, gather, inverse_pair, forward_pair, forward_one,
-    result,
-    states, terms, out_f, in_f, out_b, in_b,
-    term_send, term_recv, state_send, state_recv, f_send, f_recv, b_send, b_recv,
+    result, previous,
+    states, terms, term,
+    own_out_f, own_in_f, own_out_b, own_in_b, out_f, in_f, out_b, in_b,
+    end_send, end_recv, term_send, term_recv, state_send, state_recv,
+    own_f_send, own_f_recv, own_b_send, own_b_recv, f_send, f_recv, b_send, b_recv,
 ):
-    tables = (kxy, ky, kzx, kz, inverse, damping)
     mats = tuple(m[...] for m in (spread, gather, inverse_pair, forward_pair, forward_one))
     slot, py, pz = lax.axis_index("tm"), lax.axis_index("py"), lax.axis_index("pz")
     slices = lax.axis_size("tm")
     stride = slices // 4
-    far, core = pz // 2, pz % 2
-    is_chain = (far == 0) & (slot % stride == 0) & (slot < 2 * stride)
-    own_term = (slot == 0) & (far == 0)
+    side = slot // stride
+    is_chain = (pz == 0) & (slot % stride == 0)
+    own_term = (slot == 0) & (pz == 0)
     sends_term = jnp.logical_not(own_term) & (slot < slices - 1)
-    side = slot // stride
-    me = py * 4 + side * 2 + core
+
+    def tables_of(which):
+        return (kxy.at[which], ky.at[which], kzx, kz, inverse.at[which], damping.at[which])
+
+    def slice_device(peer):
+        return (slot, peer // 4, peer % 4)
+
+    def chain_device(peer):
+        return (peer % 4 * stride, peer // 4, 0)
 
     def term_copy(source_slice):
         return pltpu.make_async_remote_copy(
-            src_ref=payload,
+            src_ref=term,
             dst_ref=terms.at[source_slice],
             send_sem=term_send,
             recv_sem=term_recv.at[source_slice],
-            device_id=(far * stride, py, core),
+            device_id=(pz * stride, py, 0),
             device_id_type=MESH,
         )
 
@@ -434,41 +428,110 @@
             dst_ref=result,
             send_sem=state_send.at[t],
             recv_sem=state_recv,
-            device_id=(t, py, side * 2 + core),
+            device_id=(t, py, side),
             device_id_type=MESH,
         )
 
-    def part_copy(source, target, sends, recvs, owner, peer):
-        return pltpu.make_async_remote_copy(
-            src_ref=source.at[:, pl.ds(pl.multiple_of(peer * CHUNK, 8), CHUNK), :],
-            dst_ref=target.at[:, pl.ds(pl.multiple_of(owner * CHUNK, 8), CHUNK), :],
-            send_sem=sends.at[peer],
-            recv_sem=recvs.at[owner],
-            device_id=((peer // 2) % 2 * stride, peer // 4, peer % 2),
-            device_id_type=MESH,
-        )
-
-    def exchange(source, target, sends, recvs):
-        def send(j, carried):
-            peer = (me + j) % PARTS
-            part_copy(source, target, sends, recvs, me, peer).start()
-            return carried
-
-        def receive(j, carried):
-            peer = (me + PARTS - j) % PARTS
-            part_copy(source, target, sends, recvs, peer, peer).wait_recv()
-            return carried
-
-        def finish(j, carried):
-            peer = (me + j) % PARTS
-            part_copy(source, target, sends, recvs, me, peer).wait_send()
-            return carried
-
-        lax.fori_loop(1, PARTS, send, 0)
-        mine = pl.ds(pl.multiple_of(me * CHUNK, 8), CHUNK)
-        target[:, mine, :] = source[:, mine, :]
-        lax.fori_loop(1, PARTS, receive, 0)
-        lax.fori_loop(1, PARTS, finish, 0)
+    def advance_into(state, tables, me, device_of, buffers, sems, write):
+        out_f, in_f, out_b, in_b = buffers
+        f_send, f_recv, b_send, b_recv = sems
+
+        def part_copy(source, target, sends, recvs, k, owner, peer):
+            def rows(which):
+                return pl.ds(pl.multiple_of(which * CHUNK + k * 8, 8), 8)
+
+            return pltpu.make_async_remote_copy(
+                src_ref=source.at[:, rows(peer), :],
+                dst_ref=target.at[:, rows(owner), :],
+                send_sem=sends.at[k, peer],
+                recv_sem=recvs.at[k, owner],
+                device_id=device_of(peer),
+                device_id_type=MESH,
+            )
+
+        def send(source, target, sends, recvs, k):
+            def one(j, carried):
+                part_copy(source, target, sends, recvs, k, me, (me + j) % PARTS).start()
+                return carried
+
+            lax.fori_loop(1, PARTS, one, 0)
+            mine = pl.ds(pl.multiple_of(me * CHUNK + k * 8, 8), 8)
+            target[:, mine, :] = source[:, mine, :]
+
+        def receive(source, target, sends, recvs, k):
+            def one(j, carried):
+                peer = (me + PARTS - j) % PARTS
+                part_copy(source, target, sends, recvs, k, peer, peer).wait_recv()
+                return carried
+
+            lax.fori_loop(1, PARTS, one, 0)
+
+        def finish(source, target, sends, recvs, k):
+            def one(j, carried):
+                part_copy(source, target, sends, recvs, k, me, (me + j) % PARTS).wait_send()
+                return carried
+
+            lax.fori_loop(1, PARTS, one, 0)
+
+        forth = (out_f, in_f, f_send, f_recv)
+        back = (out_b, in_b, b_send, b_recv)
+        for a in range(LOCAL):
+            waves = spread_waves(state, a, tables, mats[0])
+            for g in range(3):
+                out_f[g, pl.ds(a, G, stride=LOCAL), :] = waves[:, LANES * g : LANES * (g + 1)]
+        for k in range(PIECES):
+            send(*forth, k)
+        for k in range(PIECES):
+            receive(*forth, k)
+            for x in (2 * k, 2 * k + 1):
+                made = plane_product(in_f, x, mats)
+                for g in range(2):
+                    for a in range(LOCAL):
+                        out_b[g, pl.ds(LOCAL * x + a, PARTS, stride=CHUNK), :] = made[
+                            PARTS * a : PARTS * (a + 1), LANES * g : LANES * (g + 1)
+                        ]
+            send(*back, k)
+        for k in range(PIECES):
+            finish(*forth, k)
+        for k in range(PIECES):
+            receive(*back, k)
+        for a in range(LOCAL):
+            write(a, *gather_waves(in_b, state, a, tables, mats[1]))
+        for k in range(PIECES):
+            finish(*back, k)
+
+    end_copy = pltpu.make_async_remote_copy(
+        src_ref=fine_end,
+        dst_ref=previous,
+        send_sem=end_send,
+        recv_sem=end_recv,
+        device_id=((slot + 1) % slices, py, pz),
+        device_id_type=MESH,
+    )
+
+    @pl.when(slot < slices - 1)
+    def _():
+        end_copy.start()
+
+    def write_term(a, first, third):
+        @pl.when(slot == 0)
+        def _():
+            term[a] = low[a]
+
+        @pl.when(slot != 0)
+        def _():
+            term[a, :, :LANES] = low[a, :, :LANES] - first
+            term[a, :, LANES:] = low[a, :, LANES:] - third
+
+    advance_into(
+        start,
+        tables_of(0),
+        py * 4 + pz,
+        slice_device,
+        (own_out_f, own_in_f, own_out_b, own_in_b),
+        (own_f_send, own_f_recv, own_b_send, own_b_recv),
+        write_term,
+    )
 
     @pl.when(sends_term)
     def _():
@@ -482,7 +545,7 @@
     def _():
         @pl.when(own_term)
         def _():
-            states[1] = payload[...]
+            states[1] = term[...]
 
         @pl.when(jnp.logical_not(own_term))
         def _():
@@ -491,80 +554,98 @@
 
         def step(t, carried):
             state_copy(t).start()
-            state = states.at[t]
-            for a in range(LOCAL):
-                waves = spread_waves(state, a, tables, mats[0])
-                for g in range(3):
-                    out_f[g, pl.ds(a, G, stride=LOCAL), :] = waves[:, LANES * g : LANES * (g + 1)]
-            exchange(out_f, in_f, f_send, f_recv)
-            for x in range(PLANES):
-                back = plane_product(in_f, x, mats)
-                for g in range(2):
-                    for a in range(LOCAL):
-                        out_b[g, pl.ds(LOCAL * x + a, PARTS, stride=CHUNK), :] = back[
-                            PARTS * a : PARTS * (a + 1), LANES * g : LANES * (g + 1)
-                        ]
-            exchange(out_b, in_b, b_send, b_recv)
-            term_copy(t).wait_recv()
-            for a in range(LOCAL):
-                first, third = gather_waves(in_b, state, a, tables, mats[1])
+
+            def write_state(a, first, third):
+                if a == 0:
+                    term_copy(t).wait_recv()
                 states[t + 1, a, :, :LANES] = first + terms[t, a, :, :LANES]
                 states[t + 1, a, :, LANES:] = third + terms[t, a, :, LANES:]
+
+            advance_into(
+                states.at[t],
+                tables_of(1),
+                py * 4 + side,
+                chain_device,
+                (out_f, in_f, out_b, in_b),
+                (f_send, f_recv, b_send, b_recv),
+                write_state,
+            )
             return carried
 
         lax.fori_loop(1, slices - 1, step, 0)
         state_copy(slices - 1).start()
 
-        def finish(t, carried):
+        def finish_state(t, carried):
             state_copy(t).wait_send()
             return carried
 
-        lax.fori_loop(1, slices, finish, 0)
+        lax.fori_loop(1, slices, finish_state, 0)
 
     @pl.when(sends_term)
     def _():
         term_copy(slot).wait_send()
 
+    @pl.when(slot < slices - 1)
+    def _():
+        end_copy.wait_send()
+
     @pl.when(slot != 0)
     def _():
         state_copy(slot).wait_recv()
-
-
-def chain(payload, slices):
-    core = lax.axis_index("pz") % 2
-    side = lax.axis_index("tm") // (slices // 4) % 2
-    member = lax.axis_index("py") * 4 + side * 2 + core
-    packed = payload.transpose(2, 1, 0, 3)
-    packed = jnp.concatenate([packed, packed[:, :, 2:]], axis=2).reshape(LOCAL, M, 2 * LANES)
+        end_copy.wait_recv()
+
+
+def packed_coarse(coeffs):
+    moved = coeffs.transpose(2, 1, 0, 3)
+    doubled = jnp.concatenate([moved, moved[:, :, 2:]], axis=2)
+    return doubled.reshape(LOCAL, M, 2 * LANES)
+
+
+def chain(low, start, fine_end, member, slices):
+    chain_member = lax.axis_index("py") * 4 + lax.axis_index("tm") // (slices // 4)
+    own, chained = wave_tables(member), wave_tables(chain_member)
+    stacked = [
+        one if n in (2, 3) else jnp.stack([one, two])
+        for n, (one, two) in enumerate(zip(own, chained))
+    ]
     vmem = pl.BlockSpec(memory_space=pltpu.VMEM)
-    operands = [packed, *wave_tables(member), *coarse_matrices()]
+    operands = [packed_coarse(low), packed_coarse(start), fine_end, *stacked, *coarse_matrices()]
     block = (LOCAL, M, 2 * LANES)
-    made = pl.pallas_call(
+    wide = pltpu.VMEM((3, G * LOCAL, LANES), jnp.float32)
+    narrow = pltpu.VMEM((2, G * LOCAL, LANES), jnp.float32)
+    pieces = pltpu.SemaphoreType.DMA((PIECES, PARTS))
+    anywhere = pl.BlockSpec(memory_space=pl.ANY)
+    made, previous = pl.pallas_call(
         chain_kernel,
-        out_shape=jax.ShapeDtypeStruct(block, jnp.float32),
-        in_specs=[vmem] * len(operands),
-        out_specs=vmem,
+        out_shape=(
+            jax.ShapeDtypeStruct(block, jnp.float32),
+            jax.ShapeDtypeStruct(fine_end.shape, jnp.float32),
+        ),
+        in_specs=[vmem, vmem, anywhere] + [vmem] * (len(operands) - 3),
+        out_specs=(vmem, anywhere),
         scratch_shapes=[
             pltpu.VMEM((slices,) + block, jnp.float32),
             pltpu.VMEM((slices,) + block, jnp.float32),
-            pltpu.VMEM((3, G * LOCAL, LANES), jnp.float32),
-            pltpu.VMEM((3, G * LOCAL, LANES), jnp.float32),
-            pltpu.VMEM((2, G * LOCAL, LANES), jnp.float32),
-            pltpu.VMEM((2, G * LOCAL, LANES), jnp.float32),
+            pltpu.VMEM(block, jnp.float32),
+            wide, wide, narrow, narrow,
+            wide, wide, narrow, narrow,
+            pltpu.SemaphoreType.DMA,
+            pltpu.SemaphoreType.DMA,
             pltpu.SemaphoreType.DMA,
             pltpu.SemaphoreType.DMA((slices,)),
             pltpu.SemaphoreType.DMA((slices,)),
             pltpu.SemaphoreType.DMA,
-            pltpu.SemaphoreType.DMA((PARTS,)),
-            pltpu.SemaphoreType.DMA((PARTS,)),
-            pltpu.SemaphoreType.DMA((PARTS,)),
-            pltpu.SemaphoreType.DMA((PARTS,)),
+            pieces, pieces, pieces, pieces,
+            pieces, pieces, pieces, pieces,
         ],
+        cost_estimate=pl.CostEstimate(
+            flops=10**11, bytes_accessed=10**7, transcendentals=0
+        ),
         compiler_params=pltpu.CompilerParams(
             has_side_effects=True, vmem_limit_bytes=32 * 1024 * 1024
         ),
     )(*operands)
-    return made.reshape(LOCAL, M, 4, PAIR)[:, :, :3].transpose(2, 1, 0, 3)
+    return made.reshape(LOCAL, M, 4, PAIR)[:, :, :3].transpose(2, 1, 0, 3), previous
 
 
 def shards(start_states):
@@ -580,14 +661,10 @@
     spectral_state = project(stored, wave_grid(retained, layout))
     fine_end = advance(spectral_state, "fine", layout)
     coarse_start = restrict(spectral_state, M, groups)
-    coarse_next = advance(coarse_start, "coarse", layout)
     fine_low = restrict(fine_end, M, groups)
-    correction = fine_low - coarse_next
-    payload = jnp.where(position == 0, fine_low, correction)
-    current = chain(payload, slices)
-    upper_band = fine_end - prolong(fine_low, retained, groups)
-    previous = shifted(upper_band, "tm", 1)
-    updated = prolong(current, retained, groups) + previous
+    current, previous = chain(fine_low, coarse_start, fine_end, member, slices)
+    upper_band = previous - prolong(restrict(previous, M, groups), retained, groups)
+    updated = prolong(current, retained, groups) + upper_band
     result = jnp.where(position == 0, spectral_state, updated)
     return result.reshape(1, result.shape[0], retained, result.shape[2], 1, retained)
 

time: 803 us -> 690 us (0.86)
  waiting for transfers between devices: 191 us -> 125 us
  Pallas kernels: 344 us -> 374 us
  local copies, waits for them, and re-layouts: 85.5 us -> 60 us
  matrix products: 56.8 us -> 39.7 us
  starting transfers between devices: 67.8 us -> 51.3 us
  other arithmetic: 42.8 us -> 30 us
    ppermute x1 -> x0, waiting for transfers between devices: 34.8 us -> none  [shifted(): return lax.ppermute(block, axis, route)]
    pallas_call x1, Pallas kernels: 344 us -> 374 us  [chain(): pl.pallas_call(chain_kernel, out_shape=(jax.ShapeDtypeStruct(block, jnp.f...]
    all_to_all x3 -> x2, waiting for transfers between devices: 84.2 us -> 54 us  [arrive(): lax.all_to_all(part, ('py', 'pz'), split_axis=1, concat_axis=2, tiled=True)]
    dot_general x9 -> x5, matrix products: 37.8 us -> 23.2 us  [complex_apply(): result = jnp.einsum(pattern, kernel, split, precision=highest)]
    all_to_all x3 -> x2, starting transfers between devices: 35.8 us -> 22.5 us  [arrive(): lax.all_to_all(part, ('py', 'pz'), split_axis=1, concat_axis=2, tiled=True)]
    squeeze x5 -> x0, local copies, waits for them, and re-layouts: 8.66 us -> none  [the longest x2 4.99 us: to_physical(): curl_x = rotate(wave_y * moved_x[2] - wave_z * moved_x[1])]
    reshape x5 -> x2, local copies, waits for them, and re-layouts: 19.9 us -> 11.9 us  [complex_apply(): split = values.reshape(values.shape[:-1] + (2, halfway))]
    all_to_all x2 -> x1, waiting for transfers between devices: 72.5 us -> 70.6 us  [to_spectral(): lax.all_to_all(along_y, ('py', 'pz'), split_axis=2, concat_axis=1, tiled=...]
  transfers between devices with their start and end apart: 6 -> 3, of which waited for: 6 -> 3; matrix products, arithmetic and copies ran while one was open for 3% -> 2% of each run, Pallas kernels for 0% -> 0%
where the time goes in v2:
time: 690 us; the launch traced here: 681 us
  Pallas kernels  374 us (54%)
  waiting for transfers between devices  125 us (18%)
  local copies, waits for them, and re-layouts  60 us (9%)
  starting transfers between devices  51.3 us (7%)
  matrix products  39.7 us (6%)
  other arithmetic  30 us (4%)
    pallas_call x1, Pallas kernels, chain(): pl.pallas_call(chain_kernel, out_shape=(jax.ShapeDtypeStruct(block, jnp.f...  374 us
    all_to_all x1, waiting for transfers between devices, to_spectral(): lax.all_to_all(along_y, ('py', 'pz'), split_axis=2, concat_axis=1, tiled=...  70.6 us
    all_to_all x2, waiting for transfers between devices, arrive(): lax.all_to_all(part, ('py', 'pz'), split_axis=1, concat_axis=2, tiled=True)  54 us
    all_to_all x1, starting transfers between devices, to_spectral(): lax.all_to_all(along_y, ('py', 'pz'), split_axis=2, concat_axis=1, tiled=...  28.8 us
    dot_general x5, matrix products, complex_apply(): result = jnp.einsum(pattern, kernel, split, precision=highest)  23.2 us
    all_to_all x2, starting transfers between devices, arrive(): lax.all_to_all(part, ('py', 'pz'), split_axis=1, concat_axis=2, tiled=True)  22.5 us
    unnamed x79, local copies, waits for them, and re-layouts  15.5 us
  transfers between devices with their start and end apart: 3, of which 3 were waited for; matrix products, arithmetic and copies ran while one was open for 2% of the time, Pallas kernels for 0%

profile of v2, /device:TPU:103, one launch (start us, length us, event | category | flops | bytes accessed | tf_op | source)
XLA Modules:
  0.0 681.4 jit_solution(4249704047167768387)
XLA Ops:
  0.2 1.5 fusion.158
  3.6 2.3 fusion.17
  5.9 2.3 copy-done.12
  8.4 1.7 copy.79
  10.1 9.1 %all-to-all-start.1 = ((f32[2,192,8,128]{3,2,0,1:T(8,128)}), f32[2,192,8,128]{3,2,0,1:T(8,128)}, u32[]{:S(2)}, u32[]{:S(2)}) async-start(f32[2,192,8,128]{3,2,0,1:T(8,128)} %copy.79), calls=%async_computation.1 | async-start | bytes 3145728 | tf_op jit(solution)/shard_map/all_to_all | solution.py:110
  19.2 1.9 slice-done
  21.1 2.1 copy.70
  23.2 26.1 %all-to-all-done.1 = f32[2,192,8,128]{3,2,0,1:T(8,128)} async-done(((f32[2,192,8,128]{3,2,0,1:T(8,128)}), f32[2,192,8,128]{3,2,0,1:T(8,128)}, u32[]{:S(2)}, u32[]{:S(2)}) %all-to-all-start.1) | async-done | bytes 1572896 | tf_op jit(solution)/shard_map/all_to_all | solution.py:110
  49.3 13.4 %all-to-all-start = ((f32[3,192,8,128]{3,2,0,1:T(8,128)}), f32[3,192,8,128]{3,2,0,1:T(8,128)S(1)}, u32[]{:S(2)}, u32[]{:S(2)}) async-start(f32[3,192,8,128]{3,2,0,1:T(8,128)} %copy.70), calls=%async_computation | async-start | bytes 4718592 | tf_op jit(solution)/shard_map/all_to_all | solution.py:110
  65.9 1.5 copy.80
  67.4 1.2 fusion.157
  68.7 27.9 %all-to-all-done = f32[3,192,8,128]{3,2,0,1:T(8,128)S(1)} async-done(((f32[3,192,8,128]{3,2,0,1:T(8,128)}), f32[3,192,8,128]{3,2,0,1:T(8,128)S(1)}, u32[]{:S(2)}, u32[]{:S(2)}) %all-to-all-start) | async-done | bytes 2359328 | tf_op jit(solution)/shard_map/all_to_all | solution.py:110
  98.2 1.2 bitcast_subtract_fusion.1
  99.6 1.2 pad_maximum_fusion.7
  100.8 2.3 copy.77
  103.1 3.1 slice_negate_fusion
  106.2 1.2 pad_maximum_fusion.8
  107.4 1.4 copy.82
  108.8 2.5 pad_maximum_fusion.9
  111.3 2.3 copy.84
  113.6 1.7 copy.72
  115.3 6.0 reshape.1262
  121.4 9.9 %fusion.8 = f32[3,12,64,2,192,1]{4,2,5,3,1,0:T(8,128)S(1)} fusion(f32[3,12,128,2,64,1]{4,3,2,1,0,5:T(2,128)} %bitcast.183, f32[1,2,192,128]{3,2,1,0:T(8,128)S(1)} %get-tuple-element.70, f32[1,2,192,128]{3,2,1,0:T(8,128)S(1)} %get-tuple-element.69), kind=kOutput, calls=%fused_computation.8 | convolution fusion | flops 1359052800 | bytes 6291456 | tf_op jit(solution)/shard_map/pqok,flkqh->floph/dot_general | solution.py:48
  131.3 2.0 fusion.18
  133.4 4.8 fusion.62
  138.1 4.3 fusion.64
  142.4 3.9 multiply_subtract_fusion.2
  146.3 7.4 %fusion = f32[3,12,192,128]{2,3,1,0:T(8,128)S(1)} fusion(f32[1,12,192,192]{3,2,1,0:T(8,128)} %get-tuple-element.13, f32[1,12,192,192]{3,2,1,0:T(8,128)} %get-tuple-element.12, f32[1,12,192,192]{3,2,1,0:T(8,128)} %get-tuple-element.11, s32[128]{0:T(128)S(1)} %and_select_fusion.6, pred[128]{0:T(512)(128)(4,1)S(1)} %iota_compare_fusion.3), kind=kOutput, calls=%fused_computation | convolution fusion | flops 1022164992 | bytes 8848000 | tf_op jit(solution)/shard_map/flyz,zr->flyr/dot_general | solution.py:130
  153.7 2.2 fusion.43
  156.0 2.5 copy.87
  158.5 28.8 %all-to-all-start.2 = ((f32[3,12,128,128]{3,1,0,2:T(8,128)}), f32[3,12,128,128]{3,1,0,2:T(8,128)S(1)}, u32[]{:S(2)}, u32[]{:S(2)}) async-start(f32[3,12,128,128]{3,1,0,2:T(8,128)} %copy.87), calls=%async_computation.2 | async-start | bytes 6291456 | tf_op jit(solution)/shard_map/all_to_all | solution.py:146
  192.7 1.1 multiply_exponential_fusion
  193.8 70.6 %all-to-all-done.2 = f32[3,12,128,128]{3,1,0,2:T(8,128)S(1)} async-done(((f32[3,12,128,128]{3,1,0,2:T(8,128)}), f32[3,12,128,128]{3,1,0,2:T(8,128)S(1)}, u32[]{:S(2)}, u32[]{:S(2)}) %all-to-all-start.2) | async-done | bytes 2359328 | tf_op jit(solution)/shard_map/all_to_all | solution.py:146
  264.4 2.5 copy.89
  266.9 5.9 reshape.1267
  272.7 6.7 fusion.30
  279.6 1.0 copy.92
  280.6 1.0 copy.93
  281.9 1.5 bitcast_subtract_fusion.4
  283.6 1.3 copy-done.24
  288.0 1.0 reshape.1268.low
  290.0 0.9 copy-done.3
  290.9 0.9 copy-done.4
  291.9 0.9 copy-done.5
  292.8 0.9 copy-done.6
  293.8 1.0 copy-done.7
  297.5 374.5 %shard_map.64 = (f32[4,64,256]{2,1,0:T(8,128)S(1)}, f32[3,128,8,128]{3,2,1,0:T(8,128)S(1)}) custom-call(f32[4,64,256]{2,1,0:T(8,128)S(1)} %copy-done.2, f32[4,64,256]{2,1,0:T(8,128)S(1)} %reshape.1269.start, f32[3,128,8,128]{3,2,1,0:T(8,128)S(1)} %get-tuple-element.34.fine_end, f32[2,4,64,128]{3,2,1,0:T(8,128)S(1)} %copy-done.3, ...), custom_call_target="tpu_custom_call" | custom-call | flops 99999997952 | bytes 10000000 | tf_op jit(solution)/shard_map/pallas_call | solution.py:618
  678.1 2.8 fusion.26
  (159 shorter events, 25.5 us)
Async XLA Ops:
  0.1 2.4 copy-start.34
  0.2 1.5 copy-start.26
  5.9 2.4 copy-start.12
  10.1 39.1 %all-to-all-start.1 = ((f32[2,192,8,128]{3,2,0,1:T(8,128)}), f32[2,192,8,128]{3,2,0,1:T(8,128)}, u32[]{:S(2)}, u32[]{:S(2)}) async-start(f32[2,192,8,128]{3,2,0,1:T(8,128)} %copy.79), calls=%async_computation.1 | async-start | bytes 3145728 | tf_op jit(solution)/shard_map/all_to_all | solution.py:110
  19.2 1.9 slice-start
  49.3 47.3 %all-to-all-start = ((f32[3,192,8,128]{3,2,0,1:T(8,128)}), f32[3,192,8,128]{3,2,0,1:T(8,128)S(1)}, u32[]{:S(2)}, u32[]{:S(2)}) async-start(f32[3,192,8,128]{3,2,0,1:T(8,128)} %copy.70), calls=%async_computation | async-start | bytes 4718592 | tf_op jit(solution)/shard_map/all_to_all | solution.py:110
  96.8 1.1 copy-start.22
  96.8 1.4 copy-start.23
  96.8 1.4 copy-start.31
  96.8 1.3 copy-start.38
  121.3 10.0 %copy-start.20 = (f32[12,128,128]{1,2,0:T(8,128)S(1)}, f32[12,128,128]{1,2,0:T(8,128)}, u32[]{:S(2)}) copy-start(f32[12,128,128]{1,2,0:T(8,128)} %copy.77) | copy-start | bytes 2359300
  121.3 10.0 %copy-start.21 = (f32[12,128,128]{1,2,0:T(8,128)S(1)}, f32[12,128,128]{1,2,0:T(8,128)}, u32[]{:S(2)}) copy-start(f32[12,128,128]{1,2,0:T(8,128)} %copy.84) | copy-start | bytes 2359300
  131.3 2.0 copy-start.33
  146.3 7.4 %copy-start.29 = (f32[1,2,128,192]{2,3,1,0:T(8,128)S(1)}, f32[1,2,128,192]{2,3,1,0:T(8,128)}, u32[]{:S(2)}) copy-start(f32[1,2,128,192]{2,3,1,0:T(8,128)} %get-tuple-element.67) | copy-start | bytes 589828
  146.3 7.5 %copy-start.30 = (f32[1,2,128,192]{2,3,1,0:T(8,128)S(1)}, f32[1,2,128,192]{2,3,1,0:T(8,128)}, u32[]{:S(2)}) copy-start(f32[1,2,128,192]{2,3,1,0:T(8,128)} %get-tuple-element.68) | copy-start | bytes 589828
  158.5 31.9 %copy-start.35 = (s32[128]{0:T(128)S(1)}, s32[128]{0:T(128)}, u32[]{:S(2)}) copy-start(s32[128]{0:T(128)} %copy-done.34) | copy-start | bytes 1540
  158.5 105.8 %all-to-all-start.2 = ((f32[3,12,128,128]{3,1,0,2:T(8,128)}), f32[3,12,128,128]{3,1,0,2:T(8,128)S(1)}, u32[]{:S(2)}, u32[]{:S(2)}) async-start(f32[3,12,128,128]{3,1,0,2:T(8,128)} %copy.87), calls=%async_computation.2 | async-start | bytes 6291456 | tf_op jit(solution)/shard_map/all_to_all | solution.py:146
  187.4 5.4 copy-start.27
  266.9 5.9 copy-start.28
  279.6 2.3 copy-start.13
  279.6 2.3 copy-start.32
  280.6 1.3 copy-start.25
  283.4 1.7 copy-start.18
  283.4 1.4 copy-start.24
  283.5 1.5 copy-start.14
  283.6 1.5 copy-start.16
  287.2 1.8 copy-start.10
  289.0 1.0 copy-start.2
  290.0 0.9 copy-start.3
  290.9 0.9 copy-start.4
  291.9 0.9 copy-start.5
  292.8 0.9 copy-start.6
  293.8 1.0 copy-start.7
  294.8 0.9 copy-start.8
  295.7 0.9 copy-start.9
  296.6 0.9 copy-start.11
  672.0 0.7 copy-start
  672.7 0.9 copy-start.1
  672.9 1.5 copy-start.37
  674.4 1.0 copy-start.36
  676.7 1.0 copy-start.15
  676.7 1.2 copy-start.17
  676.8 1.3 copy-start.19

commit v3 on v2

v3 whole, which is shorter than its diff:
```python
import jax
import jax.numpy as jnp
from jax import lax
from jax.experimental import pallas as pl
from jax.experimental.pallas import tpu as pltpu
import numpy as np
from jax.sharding import PartitionSpec as P

M = 64


viscosity = 0.03
time_step = 0.004


def signed_wave(places, length):
    return jnp.where(places < length // 2, places, places - length)


def restrict(coeffs, kept, groups):
    halfway = kept // 2
    retained = coeffs.shape[1]
    rows_kept = jnp.concatenate([coeffs[:, :halfway], coeffs[:, retained - halfway :]], axis=1)
    local_rows = coeffs.shape[2]
    local_kept = kept // groups // 2
    rows_kept = jnp.concatenate(
        [rows_kept[:, :, :local_kept], rows_kept[:, :, local_rows - local_kept :]], axis=2
    )
    columns_half = coeffs.shape[3] // 2
    return jnp.concatenate(
        [rows_kept[..., :halfway], rows_kept[..., columns_half : columns_half + halfway]], axis=3
    )


def prolong(coeffs, retained, groups):
    components, kept, local_kept, width = coeffs.shape
    halfway = kept // 2
    zeros_x = jnp.zeros((components, retained - kept, local_kept, width), jnp.float32)
    wider = jnp.concatenate([coeffs[:, :halfway], zeros_x, coeffs[:, halfway:]], axis=1)
    local_rows = retained // groups
    split_rows = local_kept // 2
    zeros_y = jnp.zeros((components, retained, local_rows - local_kept, width), jnp.float32)
    wider = jnp.concatenate([wider[:, :, :split_rows], zeros_y, wider[:, :, split_rows:]], axis=2)
    zeros_z = jnp.zeros((components, retained, local_rows, retained // 2 - halfway), jnp.float32)
    return jnp.concatenate([wider[..., :halfway], zeros_z, wider[..., halfway:], zeros_z], axis=3)


G = 3 * M // 2
PARTS = 16
LOCAL = M // PARTS
PLANES = G // PARTS
PIECES = PLANES // 2
FINE_LOCAL = 8
FINE_F = 5 * FINE_LOCAL
FINE_B = 3 * FINE_LOCAL
F_ROWS = 24
B_ROWS = 16
LANES = 128
PAIR = LANES // 2
QUAD = PAIR // 2
MESH = pl.DeviceIdType.MESH


def halves(matrix):
    high = np.asarray(matrix, np.float32).astype(jnp.bfloat16)
    low = (np.asarray(matrix, np.float32) - high.astype(np.float32)).astype(jnp.bfloat16)
    return high, low


def stacked(matrix, axis):
    high, low = halves(matrix)
    return jnp.asarray(np.concatenate([high, high, low], axis))


def transform_pair(retained):
    extent = 3 * retained // 2
    points = np.arange(extent)
    waves = np.where(np.arange(retained) < retained // 2, np.arange(retained), np.arange(retained) - retained)
    angle = (points[:, None] * waves[None, :]) % extent * (2.0 * np.pi / extent)
    spread = np.concatenate([np.cos(angle), np.sin(angle)], 1) * retained**-0.5
    gather = np.concatenate([np.cos(angle.T), -np.sin(angle.T)], 1) * (retained**0.5 / extent)
    return spread, gather


def depth_transforms(retained, lanes):
    extent, half = 3 * retained // 2, retained // 2
    points, harmonic = np.arange(extent), np.arange(half)
    angle = (points[:, None] * harmonic[None, :]) % extent * (2.0 * np.pi / extent)
    weight = np.where(harmonic == 0, 1.0, 2.0) * retained**-0.5
    inverse = np.zeros((retained, lanes))
    inverse[:, :extent] = np.concatenate([np.cos(angle) * weight, -np.sin(angle) * weight], 1).T
    forward = np.zeros((lanes, retained))
    forward[:extent] = np.concatenate([np.cos(angle), -np.sin(angle)], 1) * (retained**0.5 / extent)
    turned = np.concatenate([-forward[:, half:], forward[:, :half]], 1)
    return inverse, forward, turned


def coarse_matrices():
    spread, gather = transform_pair(M)
    inverse, forward, turned = depth_transforms(M, LANES)
    none_in = np.zeros_like(inverse)
    none_out = np.zeros_like(forward)
    inverse_pair = np.block([[inverse, none_in], [none_in, inverse]])
    forward_pair = np.block(
        [[forward, none_out, turned, none_out], [none_out, forward, none_out, turned]]
    )
    forward_one = np.concatenate([forward, forward, turned, turned], 1)
    order = np.concatenate([np.arange(0, G, 2), np.arange(1, G, 2)])
    gather_rows = np.concatenate([gather[:, order], gather[:, G + order]], 1)
    return [stacked(m, 1) for m in (spread, gather, spread[order], gather_rows)] + [
        stacked(m, 0) for m in (inverse_pair, forward_pair, forward_one)
    ]


def wave_tables(member):
    rows = signed_wave(jnp.arange(M, dtype=jnp.int32), M).astype(jnp.float32)[None, :, None]
    local = jnp.arange(LOCAL, dtype=jnp.int32)
    wave_y = signed_wave(local * PARTS + member, M).astype(jnp.float32)[:, None, None]
    lane = jnp.arange(LANES, dtype=jnp.int32)[None, None, :]
    wave_z = (lane % QUAD).astype(jnp.float32)
    full = (LOCAL, M, LANES)
    kx, ky, kz = (jnp.broadcast_to(w, full) for w in (rows, wave_y, wave_z))
    lower = lane < PAIR
    squared = kx * kx + ky * ky + kz * kz
    return (
        jnp.where(lower, kx, ky),
        ky,
        jnp.where(lower, kz, kx)[0],
        kz[0],
        1.0 / jnp.maximum(squared, 1.0),
        jnp.exp(-viscosity * time_step * squared),
    )


def turn(x):
    lane = lax.broadcasted_iota(jnp.int32, x.shape, 1)
    return jnp.where(
        lane % PAIR < QUAD, -pltpu.roll(x, LANES - QUAD, 1), pltpu.roll(x, QUAD, 1)
    )


def split(x):
    high = x.astype(jnp.bfloat16)
    return high, (x - high.astype(jnp.float32)).astype(jnp.bfloat16)


def left_apply(matrix, x):
    high, low = split(x)
    return jnp.dot(
        matrix, jnp.concatenate([high, low, high], 0), preferred_element_type=jnp.float32
    )


def right_apply(x, matrix):
    high, low = split(x)
    return jnp.dot(
        jnp.concatenate([high, low, high], 1), matrix, preferred_element_type=jnp.float32
    )


def spread_waves(state, a, tables, spread):
    kxy, ky, kzx, kz = tables[0][a], tables[1][a], tables[2][...], tables[3][...]
    first, third = state[a, :, :LANES], state[a, :, LANES:]
    lower = lax.broadcasted_iota(jnp.int32, first.shape, 1) < PAIR
    raw_one = ky * third - kz * first
    raw_two = kzx * first - kxy * jnp.where(lower, third, pltpu.roll(first, PAIR, 1))
    fields = jnp.concatenate(
        [first, jnp.where(lower, third, turn(raw_one)), turn(raw_two)], 1
    )
    turned = jnp.concatenate(
        [turn(first), jnp.where(lower, turn(third), -raw_one), -raw_two], 1
    )
    return left_apply(spread, jnp.concatenate([fields, turned], 0))


def plane_product(fetched, x, mats):
    spread, gather, inverse_pair, forward_pair, forward_one = mats
    fields, turned = [], []
    for g in range(3):
        rows = jnp.concatenate(
            [
                fetched[
                    pl.ds(
                        F_ROWS * (x // 2) + 8 * g + LOCAL * (x % 2) + a,
                        PARTS,
                        stride=F_ROWS * PIECES,
                    ),
                    :,
                ]
                for a in range(LOCAL)
            ],
            0,
        )
        fields.append(rows)
        turned.append(turn(rows))
    along_y = left_apply(
        spread, jnp.concatenate([jnp.concatenate(fields, 1), jnp.concatenate(turned, 1)], 0)
    )
    grids = [
        right_apply(along_y[:, LANES * g : LANES * (g + 1)], inverse_pair) for g in range(3)
    ]
    u0, u1 = grids[0][:, :LANES], grids[0][:, LANES:]
    u2, w0 = grids[1][:, :LANES], grids[1][:, LANES:]
    w1, w2 = grids[2][:, :LANES], grids[2][:, LANES:]
    pair = jnp.concatenate([u1 * w2 - u2 * w1, u2 * w0 - u0 * w2], 1)
    back_pair = right_apply(pair, forward_pair)
    back_one = right_apply(u0 * w1 - u1 * w0, forward_one)
    return left_apply(
        gather,
        jnp.concatenate(
            [
                jnp.concatenate([back_pair[:, :LANES], back_one[:, :LANES]], 1),
                jnp.concatenate([back_pair[:, LANES:], back_one[:, LANES:]], 1),
            ],
            0,
        ),
    )


def gather_waves(fetched, state, a, tables, gather):
    kxy, kz, inverse, damping = tables[0][a], tables[3][...], tables[4][a], tables[5][a]
    rows = [
        jnp.concatenate(
            [
                fetched[pl.ds(8 * g + LOCAL * h + a, G // 2, stride=B_ROWS), :]
                for h in range(2)
            ],
            0,
        )
        for g in range(2)
    ]
    turned = [turn(r) for r in rows]
    modes = left_apply(
        gather, jnp.concatenate([jnp.concatenate(rows, 1), jnp.concatenate(turned, 1)], 0)
    )
    first, third = modes[:, :LANES], modes[:, LANES:]
    along = kxy * first
    divergence = (along + pltpu.roll(along, PAIR, 1) + kz * third) * inverse
    return (
        damping * (state[a, :, :LANES] + time_step * (first - kxy * divergence)),
        damping * (state[a, :, LANES:] + time_step * (third - kz * divergence)),
    )


def chain_kernel(
    low, start, fine_end,
    kxy, ky, kzx, kz, inverse, damping,
    spread, gather, spread_rows, gather_rows, inverse_pair, forward_pair, forward_one,
    result, previous,
    states, terms, term,
    own_out_f, own_in_f, own_out_b, own_in_b, out_f, in_f, out_b, in_b,
    end_send, end_recv, term_send, term_recv, state_send, state_recv,
    own_f_send, own_f_recv, own_b_send, own_b_recv, f_send, f_recv, b_send, b_recv,
):
    mats = tuple(m[...] for m in (spread, gather, inverse_pair, forward_pair, forward_one))
    spread_x, gather_x = spread_rows[...], gather_rows[...]
    slot, py, pz = lax.axis_index("tm"), lax.axis_index("py"), lax.axis_index("pz")
    slices = lax.axis_size("tm")
    stride = slices // 4
    side = slot // stride
    is_chain = (pz == 0) & (slot % stride == 0)
    own_term = (slot == 0) & (pz == 0)
    sends_term = jnp.logical_not(own_term) & (slot < slices - 1)

    def tables_of(which):
        return (kxy.at[which], ky.at[which], kzx, kz, inverse.at[which], damping.at[which])

    def slice_device(peer):
        return (slot, peer // 4, peer % 4)

    def chain_device(peer):
        return (peer % 4 * stride, peer // 4, 0)

    def term_copy(source_slice):
        return pltpu.make_async_remote_copy(
            src_ref=term,
            dst_ref=terms.at[source_slice],
            send_sem=term_send,
            recv_sem=term_recv.at[source_slice],
            device_id=(pz * stride, py, 0),
            device_id_type=MESH,
        )

    def state_copy(t):
        return pltpu.make_async_remote_copy(
            src_ref=states.at[t],
            dst_ref=result,
            send_sem=state_send.at[t],
            recv_sem=state_recv,
            device_id=(t, py, side),
            device_id_type=MESH,
        )

    def advance_into(state, tables, me, device_of, buffers, sems, write):
        out_f, in_f, out_b, in_b = buffers
        f_send, f_recv, b_send, b_recv = sems

        def send(source, target, sends, recvs, rows, k):
            def piece(which):
                return pl.ds(pl.multiple_of((which * PIECES + k) * rows, 8), rows)

            def one(j, carried):
                peer = (me + j) % PARTS
                pltpu.make_async_remote_copy(
                    src_ref=source.at[piece(peer), :],
                    dst_ref=target.at[piece(me), :],
                    send_sem=sends.at[k],
                    recv_sem=recvs.at[k],
                    device_id=device_of(peer),
                    device_id_type=MESH,
                ).start()
                return carried

            lax.fori_loop(1, PARTS, one, 0)
            target[piece(me), :] = source[piece(me), :]

        def drain(buffer, sems, rows, k):
            bulk = buffer.at[pl.ds(0, rows * (PARTS - 1)), :]
            pltpu.make_async_copy(bulk, bulk, sems.at[k]).wait()

        forth = (out_f, in_f, f_send, f_recv, F_ROWS)
        back = (out_b, in_b, b_send, b_recv, B_ROWS)
        for a in range(LOCAL):
            waves = spread_waves(state, a, tables, spread_x)
            for g in range(3):
                for h in range(2):
                    out_f[pl.ds(8 * g + LOCAL * h + a, G // 2, stride=F_ROWS), :] = waves[
                        G // 2 * h : G // 2 * (h + 1), LANES * g : LANES * (g + 1)
                    ]
        for k in range(PIECES):
            send(*forth, k)
        for k in range(PIECES):
            drain(in_f, f_recv, F_ROWS, k)
            for x in (2 * k, 2 * k + 1):
                made = plane_product(in_f, x, mats)
                for g in range(2):
                    for a in range(LOCAL):
                        first_row = B_ROWS * k + 8 * g + LOCAL * (x % 2) + a
                        out_b[pl.ds(first_row, PARTS, stride=B_ROWS * PIECES), :] = made[
                            PARTS * a : PARTS * (a + 1), LANES * g : LANES * (g + 1)
                        ]
            send(*back, k)
        for k in range(PIECES):
            drain(out_f, f_send, F_ROWS, k)
        for k in range(PIECES):
            drain(in_b, b_recv, B_ROWS, k)
        for a in range(LOCAL):
            write(a, *gather_waves(in_b, state, a, tables, gather_x))
        for k in range(PIECES):
            drain(out_b, b_send, B_ROWS, k)

    end_copy = pltpu.make_async_remote_copy(
        src_ref=fine_end,
        dst_ref=previous,
        send_sem=end_send,
        recv_sem=end_recv,
        device_id=((slot + 1) % slices, py, pz),
        device_id_type=MESH,
    )

    def write_term(a, first, third):
        @pl.when(slot == 0)
        def _():
            term[a] = low[a]

        @pl.when(slot != 0)
        def _():
            term[a, :, :LANES] = low[a, :, :LANES] - first
            term[a, :, LANES:] = low[a, :, LANES:] - third

    advance_into(
        start,
        tables_of(0),
        py * 4 + pz,
        slice_device,
        (own_out_f, own_in_f, own_out_b, own_in_b),
        (own_f_send, own_f_recv, own_b_send, own_b_recv),
        write_term,
    )

    @pl.when(sends_term)
    def _():
        term_copy(slot).start()

    @pl.when(slot < slices - 1)
    def _():
        end_copy.start()

    @pl.when(slot == 0)
    def _():
        result[...] = jnp.zeros_like(result)

    @pl.when(is_chain)
    def _():
        @pl.when(own_term)
        def _():
            states[1] = term[...]

        @pl.when(jnp.logical_not(own_term))
        def _():
            term_copy(0).wait_recv()
            states[1] = terms[0]

        def step(t, carried):
            state_copy(t).start()

            def write_state(a, first, third):
                if a == 0:
                    term_copy(t).wait_recv()
                states[t + 1, a, :, :LANES] = first + terms[t, a, :, :LANES]
                states[t + 1, a, :, LANES:] = third + terms[t, a, :, LANES:]

            advance_into(
                states.at[t],
                tables_of(1),
                py * 4 + side,
                chain_device,
                (out_f, in_f, out_b, in_b),
                (f_send, f_recv, b_send, b_recv),
                write_state,
            )
            return carried

        lax.fori_loop(1, slices - 1, step, 0)
        state_copy(slices - 1).start()

        def finish_state(t, carried):
            state_copy(t).wait_send()
            return carried

        lax.fori_loop(1, slices, finish_state, 0)

    @pl.when(sends_term)
    def _():
        term_copy(slot).wait_send()

    @pl.when(slot < slices - 1)
    def _():
        end_copy.wait_send()

    @pl.when(slot != 0)
    def _():
        state_copy(slot).wait_recv()
        end_copy.wait_recv()


def half_turn(x):
    lane = lax.broadcasted_iota(jnp.int32, x.shape, 1)
    rolled = pltpu.roll(x, LANES // 2, 1)
    return jnp.where(lane < LANES // 2, -rolled, rolled)


def fine_kernel(
    start, spread, gather, inverse, forward,
    state, fine_end,
    out_f, in_f, out_b, in_b, f_send, f_recv, b_send, b_recv,
):
    slot, py, pz = lax.axis_index("tm"), lax.axis_index("py"), lax.axis_index("pz")
    me = py * 4 + pz
    modes = start.shape[1] // FINE_LOCAL
    planes = in_f.shape[0]
    extent = planes * PARTS
    shape = (modes, LANES)
    rows = lax.broadcasted_iota(jnp.int32, shape, 0)
    kx = jnp.where(rows < modes // 2, rows, rows - modes).astype(jnp.float32)
    kz = (lax.broadcasted_iota(jnp.int32, shape, 1) % (LANES // 2)).astype(jnp.float32)

    def wave_y(a):
        place = a * PARTS + me
        return jnp.where(place < modes // 2, place, place - modes).astype(jnp.float32)

    def without_divergence(fields, ky, squared):
        divergence = (kx * fields[0] + ky * fields[1] + kz * fields[2]) / jnp.maximum(squared, 1.0)
        return (
            fields[0] - kx * divergence,
            fields[1] - ky * divergence,
            fields[2] - kz * divergence,
        )

    for a in range(FINE_LOCAL):
        ky = wave_y(a)
        squared = kx * kx + ky * ky + kz * kz
        picked = pl.ds(a, modes, stride=FINE_LOCAL)
        fields = without_divergence([start[c, picked, :] for c in range(3)], ky, squared)
        for c in range(3):
            state[c, picked, :] = fields[c]
        turned = [half_turn(v) for v in fields]
        wide = jnp.concatenate([*fields, kx * fields[1], kx * fields[2]], 1)
        wide_turned = jnp.concatenate([*turned, kx * turned[1], kx * turned[2]], 1)
        waves = left_apply(spread[...], jnp.concatenate([wide, wide_turned], 0))
        for c in range(5):
            out_f[pl.ds(8 * c + a, extent, stride=FINE_F), :] = waves[:, LANES * c : LANES * (c + 1)]

    def device_of(peer):
        return (slot, peer // 4, peer % 4)

    def send_plane(x, carried):
        def one(j, carried):
            peer = (me + j) % PARTS
            first = pl.multiple_of((peer * planes + x) * FINE_F, 8)
            pltpu.make_async_remote_copy(
                src_ref=out_f.at[pl.ds(first, FINE_F), :],
                dst_ref=in_f.at[x, pl.ds(pl.multiple_of(me * FINE_F, 8), FINE_F), :],
                send_sem=f_send,
                recv_sem=f_recv.at[x],
                device_id=device_of(peer),
                device_id_type=MESH,
            ).start()
            return carried

        lax.fori_loop(1, PARTS, one, 0)
        mine = pl.multiple_of((me * planes + x) * FINE_F, 8)
        in_f[x, pl.ds(pl.multiple_of(me * FINE_F, 8), FINE_F), :] = out_f[pl.ds(mine, FINE_F), :]
        return carried

    lax.fori_loop(0, planes, send_plane, 0)
    places = lax.broadcasted_iota(jnp.int32, shape, 0)
    ky_rows = jnp.where(places < modes // 2, places, places - modes).astype(jnp.float32)

    def plane(x, carried):
        bulk = in_f.at[x, pl.ds(0, FINE_F * (PARTS - 1)), :]
        pltpu.make_async_copy(bulk, bulk, f_recv.at[x]).wait()
        arrived = [
            jnp.concatenate(
                [in_f[x, pl.ds(8 * c + a, PARTS, stride=FINE_F), :] for a in range(FINE_LOCAL)], 0
            )
            for c in range(5)
        ]
        raw = [
            ky_rows * arrived[2] - kz * arrived[1],
            kz * arrived[0] - arrived[4],
            arrived[3] - ky_rows * arrived[0],
        ]
        fields = jnp.concatenate(arrived[:3] + [half_turn(w) for w in raw], 1)
        turned = jnp.concatenate([half_turn(v) for v in arrived[:3]] + [-w for w in raw], 1)
        along_y = left_apply(spread[...], jnp.concatenate([fields, turned], 0))
        u0, u1, u2, w0, w1, w2 = [
            right_apply(along_y[:, LANES * c : LANES * (c + 1)], inverse[...]) for c in range(6)
        ]
        back = [
            right_apply(n, forward[...])
            for n in (u1 * w2 - u2 * w1, u2 * w0 - u0 * w2, u0 * w1 - u1 * w0)
        ]
        made = left_apply(
            gather[...],
            jnp.concatenate(
                [
                    jnp.concatenate([b[:, :LANES] for b in back], 1),
                    jnp.concatenate([b[:, LANES:] for b in back], 1),
                ],
                0,
            ),
        )
        for c in range(3):
            for a in range(FINE_LOCAL):
                out_b[x, pl.ds(8 * c + a, PARTS, stride=FINE_B), :] = made[
                    PARTS * a : PARTS * (a + 1), LANES * c : LANES * (c + 1)
                ]
        home = pl.ds(pl.multiple_of((me * planes + x) * FINE_B, 8), FINE_B)

        def one(j, carried):
            peer = (me + j) % PARTS
            pltpu.make_async_remote_copy(
                src_ref=out_b.at[x, pl.ds(pl.multiple_of(peer * FINE_B, 8), FINE_B), :],
                dst_ref=in_b.at[home, :],
                send_sem=b_send,
                recv_sem=b_recv,
                device_id=device_of(peer),
                device_id_type=MESH,
            ).start()
            return carried

        lax.fori_loop(1, PARTS, one, 0)
        in_b[home, :] = out_b[x, pl.ds(pl.multiple_of(me * FINE_B, 8), FINE_B), :]
        return carried

    lax.fori_loop(0, planes, plane, 0)
    sent = out_f.at[pl.ds(0, planes * (PARTS - 1) * FINE_F), :]
    pltpu.make_async_copy(sent, sent, f_send).wait()
    bulk = in_b.at[pl.ds(0, planes * (PARTS - 1) * FINE_B), :]
    pltpu.make_async_copy(bulk, bulk, b_recv).wait()
    for a in range(FINE_LOCAL):
        ky = wave_y(a)
        squared = kx * kx + ky * ky + kz * kz
        picked = pl.ds(a, modes, stride=FINE_LOCAL)
        columns = [in_b[pl.ds(8 * c + a, extent, stride=FINE_B), :] for c in range(3)]
        turned = [half_turn(v) for v in columns]
        narrow = left_apply(
            gather[...],
            jnp.concatenate([jnp.concatenate(columns, 1), jnp.concatenate(turned, 1)], 0),
        )
        pushed = without_divergence(
            [narrow[:, LANES * c : LANES * (c + 1)] for c in range(3)], ky, squared
        )
        damping = jnp.exp(-viscosity * time_step * squared)
        for c in range(3):
            fine_end[c, picked, :] = damping * (state[c, picked, :] + time_step * pushed[c])
    pltpu.make_async_copy(bulk, bulk, b_send).wait()


def fine_step(stored):
    retained = stored.shape[1]
    extent = 3 * retained // 2
    planes = extent // PARTS
    spread, gather = transform_pair(retained)
    inverse, forward, turned = depth_transforms(retained, 2 * LANES)
    operands = [
        stored.reshape(3, retained * FINE_LOCAL, LANES),
        stacked(spread, 1),
        stacked(gather, 1),
        stacked(inverse, 0),
        stacked(np.concatenate([forward, turned], 1), 0),
    ]
    vmem = pl.BlockSpec(memory_space=pltpu.VMEM)
    block = jax.ShapeDtypeStruct(operands[0].shape, jnp.float32)
    made = pl.pallas_call(
        fine_kernel,
        out_shape=(block, block),
        in_specs=[vmem] * len(operands),
        out_specs=(vmem, vmem),
        scratch_shapes=[
            pltpu.VMEM((extent * FINE_F, LANES), jnp.float32),
            pltpu.VMEM((planes, PARTS * FINE_F, LANES), jnp.float32),
            pltpu.VMEM((planes, PARTS * FINE_B, LANES), jnp.float32),
            pltpu.VMEM((extent * FINE_B, LANES), jnp.float32),
            pltpu.SemaphoreType.DMA,
            pltpu.SemaphoreType.DMA((planes,)),
            pltpu.SemaphoreType.DMA,
            pltpu.SemaphoreType.DMA,
        ],
        compiler_params=pltpu.CompilerParams(
            has_side_effects=True, vmem_limit_bytes=40 * 1024 * 1024
        ),
    )(*operands)
    return [one.reshape(stored.shape) for one in made]


def packed_coarse(coeffs):
    moved = coeffs.transpose(2, 1, 0, 3)
    doubled = jnp.concatenate([moved, moved[:, :, 2:]], axis=2)
    return doubled.reshape(LOCAL, M, 2 * LANES)


def chain(low, start, fine_end, member, slices):
    chain_member = lax.axis_index("py") * 4 + lax.axis_index("tm") // (slices // 4)
    own, chained = wave_tables(member), wave_tables(chain_member)
    stacked = [
        one if n in (2, 3) else jnp.stack([one, two])
        for n, (one, two) in enumerate(zip(own, chained))
    ]
    vmem = pl.BlockSpec(memory_space=pltpu.VMEM)
    operands = [packed_coarse(low), packed_coarse(start), fine_end, *stacked, *coarse_matrices()]
    block = (LOCAL, M, 2 * LANES)
    wide = pltpu.VMEM((PARTS * PIECES * F_ROWS, LANES), jnp.float32)
    narrow = pltpu.VMEM((PARTS * PIECES * B_ROWS, LANES), jnp.float32)
    pieces = pltpu.SemaphoreType.DMA((PIECES,))
    anywhere = pl.BlockSpec(memory_space=pl.ANY)
    made, previous = pl.pallas_call(
        chain_kernel,
        out_shape=(
            jax.ShapeDtypeStruct(block, jnp.float32),
            jax.ShapeDtypeStruct(fine_end.shape, jnp.float32),
        ),
        in_specs=[vmem, vmem, anywhere] + [vmem] * (len(operands) - 3),
        out_specs=(vmem, anywhere),
        scratch_shapes=[
            pltpu.VMEM((slices,) + block, jnp.float32),
            pltpu.VMEM((slices,) + block, jnp.float32),
            pltpu.VMEM(block, jnp.float32),
            wide, wide, narrow, narrow,
            wide, wide, narrow, narrow,
            pltpu.SemaphoreType.DMA,
            pltpu.SemaphoreType.DMA,
            pltpu.SemaphoreType.DMA,
            pltpu.SemaphoreType.DMA((slices,)),
            pltpu.SemaphoreType.DMA((slices,)),
            pltpu.SemaphoreType.DMA,
            pieces, pieces, pieces, pieces,
            pieces, pieces, pieces, pieces,
        ],
        cost_estimate=pl.CostEstimate(
            flops=10**11, bytes_accessed=10**7, transcendentals=0
        ),
        compiler_params=pltpu.CompilerParams(
            has_side_effects=True, vmem_limit_bytes=32 * 1024 * 1024
        ),
    )(*operands)
    return made.reshape(LOCAL, M, 4, PAIR)[:, :, :3].transpose(2, 1, 0, 3), previous


def shards(start_states):
    count_py = lax.axis_size("py")
    count_pz = lax.axis_size("pz")
    groups = count_py * count_pz
    member = lax.axis_index("py") * count_pz + lax.axis_index("pz")
    position = lax.axis_index("tm")
    slices = lax.axis_size("tm")
    retained = start_states.shape[-1]
    stored = start_states.reshape(3, retained, start_states.shape[3], retained)
    spectral_state, fine_end = fine_step(stored)
    coarse_start = restrict(spectral_state, M, groups)
    fine_low = restrict(fine_end, M, groups)
    current, previous = chain(fine_low, coarse_start, fine_end, member, slices)
    upper_band = previous - prolong(restrict(previous, M, groups), retained, groups)
    updated = prolong(current, retained, groups) + upper_band
    result = jnp.where(position == 0, spectral_state, updated)
    return result.reshape(1, result.shape[0], retained, result.shape[2], 1, retained)


def solution(mesh):
    in_specs = (P("tm", None, None, None, ("py", "pz"), None),)
    out_specs = P("tm", None, None, None, ("py", "pz"), None)
    return jax.shard_map(shards, mesh=mesh, in_specs=in_specs, out_specs=out_specs, check_vma=False)
```

time: 690 us -> 562 us (0.81); the launches traced: 681 us -> 561 us
  Pallas kernels: 374 us -> 522 us
  waiting for transfers between devices: 125 us -> 0 us
  starting transfers between devices: 51.3 us -> 0 us
  matrix products: 39.7 us -> 0 us
  local copies, waits for them, and re-layouts: 60 us -> 27.5 us
  other arithmetic: 30 us -> 11.2 us
    pallas_call x0 -> x1, Pallas kernels: none -> 160 us  [fine_step(): pl.pallas_call(fine_kernel, out_shape=(block, block), in_specs=[vmem] * l...]
    all_to_all x3 -> x0, waiting for transfers between devices: 125 us -> none  [the longest x1 70.6 us: to_spectral(): lax.all_to_all(along_y, ('py', 'pz'), split_axis=2, concat_axis=1, tiled=...]
    all_to_all x3 -> x0, starting transfers between devices: 51.3 us -> none  [the longest x1 28.8 us: to_spectral(): lax.all_to_all(along_y, ('py', 'pz'), split_axis=2, concat_axis=1, tiled=...]
    dot_general x8 -> x0, matrix products: 39.7 us -> none  [the longest x5 23.2 us: complex_apply(): result = jnp.einsum(pattern, kernel, split, precision=highest)]
    reshape x3 -> x0, local copies, waits for them, and re-layouts: 14.4 us -> none  [the longest x2 11.9 us: complex_apply(): split = values.reshape(values.shape[:-1] + (2, halfway))]
    pallas_call x1, Pallas kernels: 374 us -> 362 us  [chain(): pl.pallas_call(chain_kernel, out_shape=(jax.ShapeDtypeStruct(block, jnp.f...]
    slice x12 -> x0, local copies, waits for them, and re-layouts: 9.5 us -> none  [the longest x3 3.96 us: to_physical(): waves = arrive(moved_x[:3])]
    sub x5 -> x0, other arithmetic: 7.2 us -> none  [the longest x1 3.88 us: cross_product(): first_field[1] * second_field[2] - first_field[2] * second_field[1]]
  transfers between devices with their start and end apart: 3 -> 0, of which waited for: 3 -> 0; matrix products, arithmetic and copies ran while one was open for 2% -> 0% of each run, Pallas kernels for 0% -> 0%
where the time goes in v3:
time: 562 us; the launch traced here: 561 us
  Pallas kernels  522 us (93%)
  local copies, waits for them, and re-layouts  27.5 us (5%)
  other arithmetic  11.2 us (2%)
    pallas_call x1, Pallas kernels, chain(): pl.pallas_call(chain_kernel, out_shape=(jax.ShapeDtypeStruct(block, jnp.f...  362 us
    pallas_call x1, Pallas kernels, fine_step(): pl.pallas_call(fine_kernel, out_shape=(block, block), in_specs=[vmem] * l...  160 us
    unnamed x49, local copies, waits for them, and re-layouts  15.3 us

profile of v3, /device:TPU:103, one launch (start us, length us, event | category | flops | bytes accessed | tf_op | source)
XLA Modules:
  0.0 561.4 jit_solution(14071479529808224157)
XLA Ops:
  0.1 0.2 multiply_exponential_fusion.1
  0.3 0.9 pad_maximum_fusion.11
  1.2 0.1 broadcast_select_fusion.1
  1.3 0.7 pad_maximum_fusion.9.kxy
  2.0 0.1 broadcast_in_dim.68
  2.2 0.7 pad_maximum_fusion.10.ky
  2.9 160.0 %shard_map.118 = (f32[3,1024,128]{2,1,0:T(8,128)S(1)}, f32[3,1024,128]{2,1,0:T(8,128)S(1)}) custom-call(f32[3,1024,128]{2,1,0:T(8,128)S(1)} %bitcast.18, bf16[192,768]{1,0:T(8,128)(2,1)S(1)} %copy-done.4, bf16[128,1152]{1,0:T(8,128)(2,1)S(1)} %copy-done.5, bf16[384,256]{1,0:T(8,128)(2,1)S(1)} %copy-done.12, bf16[768,256]{1,0:T(8,128)(2,1)S(1)} %copy-done.3), custom_call_target="tpu_custom_call" | custom-call | tf_op jit(solution)/shard_map/pallas_call | solution.py:616
  163.1 0.1 fusion.7
  163.2 0.3 fusion.27
  163.5 0.3 maximum_bitcast_fusion.1
  163.8 0.1 pad_maximum_fusion.8
  163.9 1.1 copy.16
  165.0 1.4 reshape.118.start
  166.5 0.1 fusion.8
  166.6 0.3 fusion.28
  166.9 0.3 maximum_bitcast_fusion
  167.2 0.1 pad_maximum_fusion.7
  167.3 0.3 copy.15
  167.7 1.0 reshape.117.low
  168.8 1.4 copy-done.2
  170.2 0.9 copy-done.7
  171.2 0.9 copy-done.8
  172.1 0.9 copy-done.9
  173.1 0.9 copy-done.10
  174.0 0.9 copy-done.11
  175.0 1.0 copy-done.13
  176.0 0.9 copy-done.14
  176.9 0.9 copy-done.15
  177.8 0.9 copy-done.17
  178.7 0.9 copy-done.18
  179.6 0.9 copy-done.19
  180.5 362.3 %shard_map.119 = (f32[4,64,256]{2,1,0:T(8,128)S(1)}, f32[3,128,8,128]{3,2,1,0:T(8,128)S(1)}) custom-call(f32[4,64,256]{2,1,0:T(8,128)S(1)} %copy-done.7, f32[4,64,256]{2,1,0:T(8,128)S(1)} %reshape.118.start, f32[3,128,8,128]{3,2,1,0:T(8,128)S(1)} %bitcast.20, f32[2,4,64,128]{3,2,1,0:T(8,128)S(1)} %copy-done.8, f32[2,4,64,128]{3,2,1,0:T(8,128)S(1)} %copy-done.9, ...), custom_call_target="tpu_custom_call" | custom-call | flops 99999997952 | bytes 10000000 | tf_op jit(solution)/shard_map/pallas_call | solution.py:658
  542.9 0.1 fusion.6
  543.0 0.3 fusion.25
  543.3 0.2 copy-done.6
  543.5 0.7 copy-done.21
  544.2 0.9 fusion.9
  545.1 2.0 reshape.119
  547.1 1.4 copy.21
  548.6 0.4 fusion.5
  548.9 0.3 fusion.23
  549.2 0.3 fusion.24
  549.6 0.8 pad_maximum_fusion.5
  550.5 2.1 fusion.18
  552.6 2.1 fusion.20
  554.8 0.1 broadcast.291
  554.9 1.3 copy-done.20
  556.2 5.2 fusion.3
  (54 shorter events, 0.6 us)
Async XLA Ops:
  0.1 2.9 copy-start
  0.1 2.8 copy-start.3
  0.1 2.8 copy-start.4
  0.1 2.8 copy-start.5
  0.1 2.8 copy-start.12
  163.0 3.4 copy-start.1
  167.2 1.6 copy-start.16
  168.8 1.4 copy-start.2
  170.2 0.9 copy-start.7
  171.2 0.9 copy-start.8
  172.1 0.9 copy-start.9
  173.1 0.9 copy-start.10
  174.0 0.9 copy-start.11
  175.0 1.0 copy-start.13
  176.0 0.9 copy-start.14
  176.9 0.9 copy-start.15
  177.8 0.9 copy-start.17
  178.7 0.9 copy-start.18
  179.6 0.9 copy-start.19
  542.8 0.7 copy-start.6
  543.5 0.7 copy-start.21
  547.1 1.5 copy-start.22
  547.1 1.5 copy-start.23
  554.8 1.4 copy-start.20

commit v4 on v3

v4 whole, which is shorter than its diff:
```python
from functools import partial

import jax
import jax.numpy as jnp
from jax import lax
from jax.experimental import pallas as pl
from jax.experimental.pallas import tpu as pltpu
import numpy as np
from jax.sharding import PartitionSpec as P

M = 64


viscosity = 0.03
time_step = 0.004


G = 3 * M // 2
PARTS = 16
LOCAL = M // PARTS
PLANES = G // PARTS
PIECES = PLANES // 2
FINE_LOCAL = 8
FINE_F = 5 * FINE_LOCAL
FINE_B = 3 * FINE_LOCAL
F_ROWS = 24
B_ROWS = 16
LANES = 128
PAIR = LANES // 2
QUAD = PAIR // 2
MESH = pl.DeviceIdType.MESH


def halves(matrix):
    high = np.asarray(matrix, np.float32).astype(jnp.bfloat16)
    low = (np.asarray(matrix, np.float32) - high.astype(np.float32)).astype(jnp.bfloat16)
    return high, low


def stacked(matrix, axis):
    high, low = halves(matrix)
    return jnp.asarray(np.concatenate([high, high, low], axis))


def transform_pair(retained):
    extent = 3 * retained // 2
    points = np.arange(extent)
    waves = np.where(np.arange(retained) < retained // 2, np.arange(retained), np.arange(retained) - retained)
    angle = (points[:, None] * waves[None, :]) % extent * (2.0 * np.pi / extent)
    spread = np.concatenate([np.cos(angle), np.sin(angle)], 1) * retained**-0.5
    gather = np.concatenate([np.cos(angle.T), -np.sin(angle.T)], 1) * (retained**0.5 / extent)
    return spread, gather


def depth_transforms(retained, lanes):
    extent, half = 3 * retained // 2, retained // 2
    points, harmonic = np.arange(extent), np.arange(half)
    angle = (points[:, None] * harmonic[None, :]) % extent * (2.0 * np.pi / extent)
    weight = np.where(harmonic == 0, 1.0, 2.0) * retained**-0.5
    inverse = np.zeros((retained, lanes))
    inverse[:, :extent] = np.concatenate([np.cos(angle) * weight, -np.sin(angle) * weight], 1).T
    forward = np.zeros((lanes, retained))
    forward[:extent] = np.concatenate([np.cos(angle), -np.sin(angle)], 1) * (retained**0.5 / extent)
    turned = np.concatenate([-forward[:, half:], forward[:, :half]], 1)
    return inverse, forward, turned


def transforms(retained):
    spread, gather = transform_pair(M)
    inverse, forward, turned = depth_transforms(M, LANES)
    none_in = np.zeros_like(inverse)
    none_out = np.zeros_like(forward)
    inverse_pair = np.block([[inverse, none_in], [none_in, inverse]])
    forward_pair = np.block(
        [[forward, none_out, turned, none_out], [none_out, forward, none_out, turned]]
    )
    forward_one = np.concatenate([forward, forward, turned, turned], 1)
    order = np.concatenate([np.arange(0, G, 2), np.arange(1, G, 2)])
    gather_rows = np.concatenate([gather[:, order], gather[:, G + order]], 1)
    fine_spread, fine_gather = transform_pair(retained)
    fine_inverse, fine_forward, fine_turned = depth_transforms(retained, 2 * LANES)
    fine_back = np.concatenate([fine_forward, fine_turned], 1)
    deep = [stacked(m, 0) for m in (fine_inverse, fine_back, inverse_pair, forward_pair, forward_one)]
    edges = np.cumsum([0] + [m.shape[0] for m in deep]).tolist()
    operands = [
        stacked(fine_spread, 1),
        stacked(fine_gather, 1),
        jnp.concatenate(deep, 0),
        jnp.concatenate([stacked(spread, 1), stacked(spread[order], 1)], 0),
        jnp.concatenate([stacked(gather, 1), stacked(gather_rows, 1)], 0),
    ]
    return operands, edges


def turn(x):
    lane = lax.broadcasted_iota(jnp.int32, x.shape, 1)
    return jnp.where(
        lane % PAIR < QUAD, -pltpu.roll(x, LANES - QUAD, 1), pltpu.roll(x, QUAD, 1)
    )


def split(x):
    high = x.astype(jnp.bfloat16)
    return high, (x - high.astype(jnp.float32)).astype(jnp.bfloat16)


def left_apply(matrix, x):
    high, low = split(x)
    return jnp.dot(
        matrix, jnp.concatenate([high, low, high], 0), preferred_element_type=jnp.float32
    )


def right_apply(x, matrix):
    high, low = split(x)
    return jnp.dot(
        jnp.concatenate([high, low, high], 1), matrix, preferred_element_type=jnp.float32
    )


def spread_waves(state, a, tables, spread):
    kx, ky, kz = tables[0], tables[1](a), tables[2]
    first, third = state[a, :, :LANES], state[a, :, LANES:]
    lower = lax.broadcasted_iota(jnp.int32, first.shape, 1) < PAIR
    kxy, kzx = jnp.where(lower, kx, ky), jnp.where(lower, kz, kx)
    raw_one = ky * third - kz * first
    raw_two = kzx * first - kxy * jnp.where(lower, third, pltpu.roll(first, PAIR, 1))
    fields = jnp.concatenate(
        [first, jnp.where(lower, third, turn(raw_one)), turn(raw_two)], 1
    )
    turned = jnp.concatenate(
        [turn(first), jnp.where(lower, turn(third), -raw_one), -raw_two], 1
    )
    return left_apply(spread, jnp.concatenate([fields, turned], 0))


def plane_product(fetched, x, mats):
    spread, gather, inverse_pair, forward_pair, forward_one = mats
    fields, turned = [], []
    for g in range(3):
        rows = jnp.concatenate(
            [
                fetched[
                    pl.ds(
                        F_ROWS * (x // 2) + 8 * g + LOCAL * (x % 2) + a,
                        PARTS,
                        stride=F_ROWS * PIECES,
                    ),
                    :,
                ]
                for a in range(LOCAL)
            ],
            0,
        )
        fields.append(rows)
        turned.append(turn(rows))
    along_y = left_apply(
        spread, jnp.concatenate([jnp.concatenate(fields, 1), jnp.concatenate(turned, 1)], 0)
    )
    grids = [
        right_apply(along_y[:, LANES * g : LANES * (g + 1)], inverse_pair) for g in range(3)
    ]
    u0, u1 = grids[0][:, :LANES], grids[0][:, LANES:]
    u2, w0 = grids[1][:, :LANES], grids[1][:, LANES:]
    w1, w2 = grids[2][:, :LANES], grids[2][:, LANES:]
    pair = jnp.concatenate([u1 * w2 - u2 * w1, u2 * w0 - u0 * w2], 1)
    back_pair = right_apply(pair, forward_pair)
    back_one = right_apply(u0 * w1 - u1 * w0, forward_one)
    return left_apply(
        gather,
        jnp.concatenate(
            [
                jnp.concatenate([back_pair[:, :LANES], back_one[:, :LANES]], 1),
                jnp.concatenate([back_pair[:, LANES:], back_one[:, LANES:]], 1),
            ],
            0,
        ),
    )


def gather_waves(fetched, state, a, tables, gather):
    kx, ky, kz, inverse, damping = tables[0], tables[1](a), tables[2], tables[3][a], tables[4][a]
    kxy = jnp.where(lax.broadcasted_iota(jnp.int32, kx.shape, 1) < PAIR, kx, ky)
    rows = [
        jnp.concatenate(
            [
                fetched[pl.ds(8 * g + LOCAL * h + a, G // 2, stride=B_ROWS), :]
                for h in range(2)
            ],
            0,
        )
        for g in range(2)
    ]
    turned = [turn(r) for r in rows]
    modes = left_apply(
        gather, jnp.concatenate([jnp.concatenate(rows, 1), jnp.concatenate(turned, 1)], 0)
    )
    first, third = modes[:, :LANES], modes[:, LANES:]
    along = kxy * first
    divergence = (along + pltpu.roll(along, PAIR, 1) + kz * third) * inverse
    return (
        damping * (state[a, :, :LANES] + time_step * (first - kxy * divergence)),
        damping * (state[a, :, LANES:] + time_step * (third - kz * divergence)),
    )


def half_turn(x):
    lane = lax.broadcasted_iota(jnp.int32, x.shape, 1)
    rolled = pltpu.roll(x, LANES // 2, 1)
    return jnp.where(lane < LANES // 2, -rolled, rolled)


def pack_pair(first, second):
    lane = lax.broadcasted_iota(jnp.int32, first.shape, 1)
    lower = jnp.where(lane < QUAD, first, pltpu.roll(first, LANES - QUAD, 1))
    upper = jnp.where(lane < LANES - QUAD, pltpu.roll(second, PAIR, 1), pltpu.roll(second, QUAD, 1))
    return jnp.where(lane < PAIR, lower, upper)


def kept_rows(x):
    return jnp.concatenate([x[: M // 2], x[x.shape[0] - M // 2 :]], 0)


def iteration_kernel(
    edges,
    start, fine_spread, fine_gather, deep, coarse_spread, coarse_gather,
    result,
    state, fine_end, fine_out_f, fine_in_f, fine_out_b, fine_in_b,
    coarse_start, inverses, dampings, states, terms, term, landed,
    own_out_f, own_in_f, own_out_b, own_in_b, out_f, in_f, out_b, in_b,
    fine_f_send, fine_f_recv, fine_b_send, fine_b_recv,
    end_send, end_recv, term_send, term_recv, state_send, state_recv,
    own_f_send, own_f_recv, own_b_send, own_b_recv, f_send, f_recv, b_send, b_recv,
):
    slot, py, pz = lax.axis_index("tm"), lax.axis_index("py"), lax.axis_index("pz")
    slices = lax.axis_size("tm")
    stride = slices // 4
    side = slot // stride
    me = py * 4 + pz
    is_chain = (pz == 0) & (slot % stride == 0)
    own_term = (slot == 0) & (pz == 0)
    sends_term = jnp.logical_not(own_term) & (slot < slices - 1)
    fine_inverse, fine_back, inverse_pair, forward_pair, forward_one = [
        deep.at[pl.ds(low, high - low), :] for low, high in zip(edges, edges[1:])
    ]
    points, kept = G, M
    mats = (
        coarse_spread[:points], coarse_gather[:kept],
        inverse_pair[...], forward_pair[...], forward_one[...],
    )
    spread_x, gather_x = coarse_spread[points:], coarse_gather[kept:]

    def place_wave(place, length):
        return jnp.where(place < length // 2, place, place - length).astype(jnp.float32)

    coarse_shape = (M, LANES)
    coarse_kx = place_wave(lax.broadcasted_iota(jnp.int32, coarse_shape, 0), M)
    coarse_kz = (lax.broadcasted_iota(jnp.int32, coarse_shape, 1) % QUAD).astype(jnp.float32)
    members = (me, py * 4 + side)

    def coarse_ky(which):
        return lambda a: place_wave(a * PARTS + members[which], M)

    def tables_of(which):
        return (coarse_kx, coarse_ky(which), coarse_kz, inverses.at[which], dampings.at[which])

    for which in range(2):
        for a in range(LOCAL):
            ky = coarse_ky(which)(a)
            squared = coarse_kx * coarse_kx + ky * ky + coarse_kz * coarse_kz
            inverses[which, a] = 1.0 / jnp.maximum(squared, 1.0)
            dampings[which, a] = jnp.exp(-viscosity * time_step * squared)

    def slice_device(peer):
        return (slot, peer // 4, peer % 4)

    def chain_device(peer):
        return (peer % 4 * stride, peer // 4, 0)

    def for_peers(who, act):
        def some(i, carried):
            for u in range(5):
                act((who + 1 + 5 * i + u) % PARTS)
            return carried

        lax.fori_loop(0, 3, some, 0)

    def term_copy(source_slice):
        return pltpu.make_async_remote_copy(
            src_ref=term,
            dst_ref=terms.at[source_slice],
            send_sem=term_send,
            recv_sem=term_recv.at[source_slice],
            device_id=(pz * stride, py, 0),
            device_id_type=MESH,
        )

    def state_copy(t):
        return pltpu.make_async_remote_copy(
            src_ref=states.at[t],
            dst_ref=landed,
            send_sem=state_send.at[t],
            recv_sem=state_recv,
            device_id=(t, py, side),
            device_id_type=MESH,
        )

    def advance_parts(state, tables, me, device_of, buffers, sems, write):
        out_f, in_f, out_b, in_b = buffers
        f_send, f_recv, b_send, b_recv = sems

        def send(source, target, sends, recvs, rows, k):
            def piece(which):
                return pl.ds(pl.multiple_of((which * PIECES + k) * rows, 8), rows)

            def one(peer):
                pltpu.make_async_remote_copy(
                    src_ref=source.at[piece(peer), :],
                    dst_ref=target.at[piece(me), :],
                    send_sem=sends.at[k],
                    recv_sem=recvs.at[k],
                    device_id=device_of(peer),
                    device_id_type=MESH,
                ).start()

            for_peers(me, one)
            target[piece(me), :] = source[piece(me), :]

        def drain(buffer, sems, rows, k):
            bulk = buffer.at[pl.ds(0, rows * (PARTS - 1)), :]
            pltpu.make_async_copy(bulk, bulk, sems.at[k]).wait()

        forth = (out_f, in_f, f_send, f_recv, F_ROWS)
        back = (out_b, in_b, b_send, b_recv, B_ROWS)
        def begin():
            for a in range(LOCAL):
                waves = spread_waves(state, a, tables, spread_x)
                for g in range(3):
                    for h in range(2):
                        out_f[pl.ds(8 * g + LOCAL * h + a, G // 2, stride=F_ROWS), :] = waves[
                            G // 2 * h : G // 2 * (h + 1), LANES * g : LANES * (g + 1)
                        ]
            for k in range(PIECES):
                send(*forth, k)

        def middle():
            for k in range(PIECES):
                drain(in_f, f_recv, F_ROWS, k)
                for x in (2 * k, 2 * k + 1):
                    made = plane_product(in_f, x, mats)
                    for g in range(2):
                        for a in range(LOCAL):
                            first_row = B_ROWS * k + 8 * g + LOCAL * (x % 2) + a
                            out_b[pl.ds(first_row, PARTS, stride=B_ROWS * PIECES), :] = made[
                                PARTS * a : PARTS * (a + 1), LANES * g : LANES * (g + 1)
                            ]
                send(*back, k)

        def end():
            for k in range(PIECES):
                drain(out_f, f_send, F_ROWS, k)
            for k in range(PIECES):
                drain(in_b, b_recv, B_ROWS, k)
            for a in range(LOCAL):
                write(a, *gather_waves(in_b, state, a, tables, gather_x))
            for k in range(PIECES):
                drain(out_b, b_send, B_ROWS, k)

        return begin, middle, end

    def write_own(a, first, third):
        term[a, :, :LANES] = first
        term[a, :, LANES:] = third

    own_begin, own_middle, own_end = advance_parts(
        coarse_start,
        tables_of(0),
        me,
        slice_device,
        (own_out_f, own_in_f, own_out_b, own_in_b),
        (own_f_send, own_f_recv, own_b_send, own_b_recv),
        write_own,
    )

    modes = start.shape[1] // FINE_LOCAL
    planes = fine_in_f.shape[0]
    extent = planes * PARTS
    shape = (modes, LANES)
    rows = lax.broadcasted_iota(jnp.int32, shape, 0)
    kx = jnp.where(rows < modes // 2, rows, rows - modes).astype(jnp.float32)
    kz = (lax.broadcasted_iota(jnp.int32, shape, 1) % (LANES // 2)).astype(jnp.float32)

    def wave_y(a):
        place = a * PARTS + me
        return jnp.where(place < modes // 2, place, place - modes).astype(jnp.float32)

    def without_divergence(fields, ky, squared):
        divergence = (kx * fields[0] + ky * fields[1] + kz * fields[2]) / jnp.maximum(squared, 1.0)
        return (
            fields[0] - kx * divergence,
            fields[1] - ky * divergence,
            fields[2] - kz * divergence,
        )

    kept_places = (*range(LOCAL // 2), *range(FINE_LOCAL - LOCAL // 2, FINE_LOCAL))
    for a in range(FINE_LOCAL):
        ky = wave_y(a)
        squared = kx * kx + ky * ky + kz * kz
        picked = pl.ds(a, modes, stride=FINE_LOCAL)
        fields = without_divergence([start[c, picked, :] for c in range(3)], ky, squared)
        for c in range(3):
            state[c, picked, :] = fields[c]
        if a in kept_places:
            slim = [kept_rows(v) for v in fields]
            coarse_start[kept_places.index(a), :, :LANES] = pack_pair(slim[0], slim[1])
            coarse_start[kept_places.index(a), :, LANES:] = pack_pair(slim[2], slim[2])
        turned = [half_turn(v) for v in fields]
        wide = jnp.concatenate([*fields, kx * fields[1], kx * fields[2]], 1)
        wide_turned = jnp.concatenate([*turned, kx * turned[1], kx * turned[2]], 1)
        waves = left_apply(fine_spread[...], jnp.concatenate([wide, wide_turned], 0))
        for c in range(5):
            fine_out_f[pl.ds(8 * c + a, extent, stride=FINE_F), :] = waves[:, LANES * c : LANES * (c + 1)]

    def send_plane(x, carried):
        def one(peer):
            first = pl.multiple_of((peer * planes + x) * FINE_F, 8)
            pltpu.make_async_remote_copy(
                src_ref=fine_out_f.at[pl.ds(first, FINE_F), :],
                dst_ref=fine_in_f.at[x, pl.ds(pl.multiple_of(me * FINE_F, 8), FINE_F), :],
                send_sem=fine_f_send,
                recv_sem=fine_f_recv.at[x],
                device_id=slice_device(peer),
                device_id_type=MESH,
            ).start()

        for_peers(me, one)
        mine = pl.multiple_of((me * planes + x) * FINE_F, 8)
        fine_in_f[x, pl.ds(pl.multiple_of(me * FINE_F, 8), FINE_F), :] = fine_out_f[pl.ds(mine, FINE_F), :]
        return carried

    own_begin()
    lax.fori_loop(0, planes, send_plane, 0)
    own_middle()
    places = lax.broadcasted_iota(jnp.int32, shape, 0)
    ky_rows = jnp.where(places < modes // 2, places, places - modes).astype(jnp.float32)

    def plane(x, carried):
        bulk = fine_in_f.at[x, pl.ds(0, FINE_F * (PARTS - 1)), :]
        pltpu.make_async_copy(bulk, bulk, fine_f_recv.at[x]).wait()
        arrived = [
            jnp.concatenate(
                [fine_in_f[x, pl.ds(8 * c + a, PARTS, stride=FINE_F), :] for a in range(FINE_LOCAL)], 0
            )
            for c in range(5)
        ]
        raw = [
            ky_rows * arrived[2] - kz * arrived[1],
            kz * arrived[0] - arrived[4],
            arrived[3] - ky_rows * arrived[0],
        ]
        fields = jnp.concatenate(arrived[:3] + [half_turn(w) for w in raw], 1)
        turned = jnp.concatenate([half_turn(v) for v in arrived[:3]] + [-w for w in raw], 1)
        along_y = left_apply(fine_spread[...], jnp.concatenate([fields, turned], 0))
        u0, u1, u2, w0, w1, w2 = [
            right_apply(along_y[:, LANES * c : LANES * (c + 1)], fine_inverse[...]) for c in range(6)
        ]
        back = [
            right_apply(n, fine_back[...])
            for n in (u1 * w2 - u2 * w1, u2 * w0 - u0 * w2, u0 * w1 - u1 * w0)
        ]
        made = left_apply(
            fine_gather[...],
            jnp.concatenate(
                [
                    jnp.concatenate([b[:, :LANES] for b in back], 1),
                    jnp.concatenate([b[:, LANES:] for b in back], 1),
                ],
                0,
            ),
        )
        for c in range(3):
            for a in range(FINE_LOCAL):
                fine_out_b[x, pl.ds(8 * c + a, PARTS, stride=FINE_B), :] = made[
                    PARTS * a : PARTS * (a + 1), LANES * c : LANES * (c + 1)
                ]
        home = pl.ds(pl.multiple_of((me * planes + x) * FINE_B, 8), FINE_B)

        def one(peer):
            pltpu.make_async_remote_copy(
                src_ref=fine_out_b.at[x, pl.ds(pl.multiple_of(peer * FINE_B, 8), FINE_B), :],
                dst_ref=fine_in_b.at[home, :],
                send_sem=fine_b_send,
                recv_sem=fine_b_recv,
                device_id=slice_device(peer),
                device_id_type=MESH,
            ).start()

        for_peers(me, one)
        fine_in_b[home, :] = fine_out_b[x, pl.ds(pl.multiple_of(me * FINE_B, 8), FINE_B), :]
        return carried

    lax.fori_loop(0, planes, plane, 0)
    own_end()
    sent = fine_out_f.at[pl.ds(0, planes * (PARTS - 1) * FINE_F), :]
    pltpu.make_async_copy(sent, sent, fine_f_send).wait()
    bulk = fine_in_b.at[pl.ds(0, planes * (PARTS - 1) * FINE_B), :]
    pltpu.make_async_copy(bulk, bulk, fine_b_recv).wait()
    for a in range(FINE_LOCAL):
        ky = wave_y(a)
        squared = kx * kx + ky * ky + kz * kz
        picked = pl.ds(a, modes, stride=FINE_LOCAL)
        columns = [fine_in_b[pl.ds(8 * c + a, extent, stride=FINE_B), :] for c in range(3)]
        turned = [half_turn(v) for v in columns]
        narrow = left_apply(
            fine_gather[...],
            jnp.concatenate([jnp.concatenate(columns, 1), jnp.concatenate(turned, 1)], 0),
        )
        pushed = without_divergence(
            [narrow[:, LANES * c : LANES * (c + 1)] for c in range(3)], ky, squared
        )
        damping = jnp.exp(-viscosity * time_step * squared)
        ends = [damping * (state[c, picked, :] + time_step * pushed[c]) for c in range(3)]
        for c in range(3):
            fine_end[c, picked, :] = ends[c]
        if a in kept_places:
            place = kept_places.index(a)
            slim = [kept_rows(v) for v in ends]
            for half, low in ((0, pack_pair(slim[0], slim[1])), (LANES, pack_pair(slim[2], slim[2]))):
                lanes = pl.ds(half, LANES)
                term[place, :, lanes] = low - jnp.where(slot == 0, 0.0, term[place, :, lanes])
    pltpu.make_async_copy(bulk, bulk, fine_b_send).wait()

    end_copy = pltpu.make_async_remote_copy(
        src_ref=fine_end,
        dst_ref=result,
        send_sem=end_send,
        recv_sem=end_recv,
        device_id=((slot + 1) % slices, py, pz),
        device_id_type=MESH,
    )

    @pl.when(sends_term)
    def _():
        term_copy(slot).start()

    @pl.when(slot < slices - 1)
    def _():
        end_copy.start()

    @pl.when(is_chain)
    def _():
        @pl.when(own_term)
        def _():
            states[1] = term[...]

        @pl.when(jnp.logical_not(own_term))
        def _():
            term_copy(0).wait_recv()
            states[1] = terms[0]

        def step(t, carried):
            state_copy(t).start()

            def write_state(a, first, third):
                if a == 0:
                    term_copy(t).wait_recv()
                states[t + 1, a, :, :LANES] = first + terms[t, a, :, :LANES]
                states[t + 1, a, :, LANES:] = third + terms[t, a, :, LANES:]

            begin, middle, end = advance_parts(
                states.at[t],
                tables_of(1),
                members[1],
                chain_device,
                (out_f, in_f, out_b, in_b),
                (f_send, f_recv, b_send, b_recv),
                write_state,
            )
            begin()
            middle()
            end()
            return carried

        lax.fori_loop(1, slices - 1, step, 0)
        state_copy(slices - 1).start()

        def finish_state(t, carried):
            state_copy(t).wait_send()
            return carried

        lax.fori_loop(1, slices, finish_state, 0)

    @pl.when(sends_term)
    def _():
        term_copy(slot).wait_send()

    @pl.when(slot < slices - 1)
    def _():
        end_copy.wait_send()

    @pl.when(slot == 0)
    def _():
        result[...] = state[...]

    @pl.when(slot != 0)
    def _():
        state_copy(slot).wait_recv()
        end_copy.wait_recv()
        half = M // 2
        lane = lax.broadcasted_iota(jnp.int32, (half, LANES), 1)
        real, imaginary = lane < QUAD, (lane >= PAIR) & (lane < PAIR + QUAD)
        for place, a in enumerate(kept_places):
            for top, first in ((0, 0), (half, modes - half)):
                pair = landed[place, pl.ds(top, half), :LANES]
                single = landed[place, pl.ds(top, half), LANES:]
                moved = (
                    (pair, pltpu.roll(pair, QUAD, 1)),
                    (pltpu.roll(pair, PAIR, 1), pltpu.roll(pair, LANES - QUAD, 1)),
                    (single, pltpu.roll(single, QUAD, 1)),
                )
                rows = pl.ds(first * FINE_LOCAL + a, half, stride=FINE_LOCAL)
                for c in range(3):
                    result[c, rows, :] = jnp.where(
                        real, moved[c][0], jnp.where(imaginary, moved[c][1], result[c, rows, :])
                    )


def shards(start_states):
    retained = start_states.shape[-1]
    extent = 3 * retained // 2
    planes = extent // PARTS
    slices = lax.axis_size("tm")
    matrices, edges = transforms(retained)
    operands = [start_states.reshape(3, retained * FINE_LOCAL, LANES), *matrices]
    vmem = pl.BlockSpec(memory_space=pltpu.VMEM)

    def floats(*shape):
        return pltpu.VMEM(shape, jnp.float32)

    block = (LOCAL, M, 2 * LANES)
    wide = floats(PARTS * PIECES * F_ROWS, LANES)
    narrow = floats(PARTS * PIECES * B_ROWS, LANES)
    single = pltpu.SemaphoreType.DMA
    pieces = pltpu.SemaphoreType.DMA((PIECES,))
    each = pltpu.SemaphoreType.DMA((slices,))
    result = pl.pallas_call(
        partial(iteration_kernel, edges),
        out_shape=jax.ShapeDtypeStruct(operands[0].shape, jnp.float32),
        in_specs=[vmem] * len(operands),
        out_specs=vmem,
        scratch_shapes=[
            floats(*operands[0].shape), floats(*operands[0].shape),
            floats(extent * FINE_F, LANES), floats(planes, PARTS * FINE_F, LANES),
            floats(planes, PARTS * FINE_B, LANES), floats(extent * FINE_B, LANES),
            floats(*block), floats(2, LOCAL, M, LANES), floats(2, LOCAL, M, LANES),
            floats(slices, *block), floats(slices, *block), floats(*block), floats(*block),
            wide, wide, narrow, narrow, wide, wide, narrow, narrow,
            single, pltpu.SemaphoreType.DMA((planes,)), single, single,
            single, single, single, each, each, single,
            pieces, pieces, pieces, pieces, pieces, pieces, pieces, pieces,
        ],
        compiler_params=pltpu.CompilerParams(
            has_side_effects=True, vmem_limit_bytes=56 * 1024 * 1024
        ),
    )(*operands)
    return result.reshape(start_states.shape)


def solution(mesh):
    in_specs = (P("tm", None, None, None, ("py", "pz"), None),)
    out_specs = P("tm", None, None, None, ("py", "pz"), None)
    return jax.shard_map(shards, mesh=mesh, in_specs=in_specs, out_specs=out_specs, check_vma=False)
```

time: 562 us -> 507 us (0.902)
  local copies, waits for them, and re-layouts: 27.5 us -> 3.63 us
  Pallas kernels: 522 us -> 504 us
  other arithmetic: 11.2 us -> 0 us
    pallas_call x2 -> x1, Pallas kernels: 522 us -> 504 us  [shards(): pl.pallas_call(partial(iteration_kernel, edges), out_shape=jax.ShapeDtype...]
    unnamed x49 -> x1, local copies, waits for them, and re-layouts: 15.3 us -> 3.63 us
    slice x13 -> x0, local copies, waits for them, and re-layouts: 5.92 us -> none  [the longest x2 4.29 us: prolong(): wider[..., :halfway]]
where the time goes in v4:
time: 507 us
  Pallas kernels  504 us (99%)
    pallas_call x1, Pallas kernels, shards(): pl.pallas_call(partial(iteration_kernel, edges), out_shape=jax.ShapeDtype...  504 us

profile of v4, /device:TPU:103, one launch (start us, length us, event | category | flops | bytes accessed | tf_op | source)
XLA Modules:
  0.0 507.3 jit_solution(3182654229754579705)
XLA Ops:
  0.0 503.6 %shard_map.118 = f32[3,1024,128]{2,1,0:T(8,128)} custom-call(f32[3,1024,128]{2,1,0:T(8,128)} %bitcast.5, bf16[192,768]{1,0:T(8,128)(2,1)} %constant.27.clone.fine_spread, bf16[128,1152]{1,0:T(8,128)(2,1)} %constant.28.clone.fine_gather, bf16[2688,256]{1,0:T(8,128)(2,1)} %constant.34.deep, bf16[192,384]{1,0:T(8,128)(2,1)} %constant.35.coarse_spread, ...), custom_call_target="tpu_custom_call" | custom-call | tf_op jit(solution)/shard_map/pallas_call | solution.py:646
  503.6 3.6 copy.15

commit v5 on v4

--- a/solution.py
+++ b/solution.py
@@ -134,7 +134,7 @@
     return left_apply(spread, jnp.concatenate([fields, turned], 0))
 
 
-def plane_product(fetched, x, mats):
+def plane_product(fetched, k, h, mats):
     spread, gather, inverse_pair, forward_pair, forward_one = mats
     fields, turned = [], []
     for g in range(3):
@@ -142,7 +142,7 @@
             [
                 fetched[
                     pl.ds(
-                        F_ROWS * (x // 2) + 8 * g + LOCAL * (x % 2) + a,
+                        F_ROWS * k + 8 * g + LOCAL * h + a,
                         PARTS,
                         stride=F_ROWS * PIECES,
                     ),
@@ -277,13 +277,13 @@
     def chain_device(peer):
         return (peer % 4 * stride, peer // 4, 0)
 
-    def for_peers(who, act):
+    def for_peers(who, act, once=5):
         def some(i, carried):
-            for u in range(5):
-                act((who + 1 + 5 * i + u) % PARTS)
+            for u in range(once):
+                act((who + 1 + once * i + u) % PARTS)
             return carried
 
-        lax.fori_loop(0, 3, some, 0)
+        lax.fori_loop(0, (PARTS - 1) // once, some, 0)
 
     def term_copy(source_slice):
         return pltpu.make_async_remote_copy(
@@ -305,7 +305,7 @@
             device_id_type=MESH,
         )
 
-    def advance_parts(state, tables, me, device_of, buffers, sems, write):
+    def advance_parts(state, tables, me, device_of, buffers, sems, write, compact):
         out_f, in_f, out_b, in_b = buffers
         f_send, f_recv, b_send, b_recv = sems
 
@@ -323,7 +323,7 @@
                     device_id_type=MESH,
                 ).start()
 
-            for_peers(me, one)
+            for_peers(me, one, 1 if compact else 5)
             target[piece(me), :] = source[piece(me), :]
 
         def drain(buffer, sems, rows, k):
@@ -343,18 +343,28 @@
             for k in range(PIECES):
                 send(*forth, k)
 
+        def piece_work(k):
+            drain(in_f, f_recv, F_ROWS, k)
+            for h in range(2):
+                made = plane_product(in_f, k, h, mats)
+                for g in range(2):
+                    for a in range(LOCAL):
+                        first_row = B_ROWS * k + 8 * g + LOCAL * h + a
+                        out_b[pl.ds(first_row, PARTS, stride=B_ROWS * PIECES), :] = made[
+                            PARTS * a : PARTS * (a + 1), LANES * g : LANES * (g + 1)
+                        ]
+            send(*back, k)
+
         def middle():
-            for k in range(PIECES):
-                drain(in_f, f_recv, F_ROWS, k)
-                for x in (2 * k, 2 * k + 1):
-                    made = plane_product(in_f, x, mats)
-                    for g in range(2):
-                        for a in range(LOCAL):
-                            first_row = B_ROWS * k + 8 * g + LOCAL * (x % 2) + a
-                            out_b[pl.ds(first_row, PARTS, stride=B_ROWS * PIECES), :] = made[
-                                PARTS * a : PARTS * (a + 1), LANES * g : LANES * (g + 1)
-                            ]
-                send(*back, k)
+            if compact:
+                def turn_of(k, carried):
+                    piece_work(k)
+                    return carried
+
+                lax.fori_loop(0, PIECES, turn_of, 0)
+            else:
+                for k in range(PIECES):
+                    piece_work(k)
 
         def end():
             for k in range(PIECES):
@@ -380,6 +390,7 @@
         (own_out_f, own_in_f, own_out_b, own_in_b),
         (own_f_send, own_f_recv, own_b_send, own_b_recv),
         write_own,
+        compact=True,
     )
 
     modes = start.shape[1] // FINE_LOCAL
@@ -433,7 +444,7 @@
                 device_id_type=MESH,
             ).start()
 
-        for_peers(me, one)
+        for_peers(me, one, 3)
         mine = pl.multiple_of((me * planes + x) * FINE_F, 8)
         fine_in_f[x, pl.ds(pl.multiple_of(me * FINE_F, 8), FINE_F), :] = fine_out_f[pl.ds(mine, FINE_F), :]
         return carried
@@ -495,7 +506,7 @@
                 device_id_type=MESH,
             ).start()
 
-        for_peers(me, one)
+        for_peers(me, one, 3)
         fine_in_b[home, :] = fine_out_b[x, pl.ds(pl.multiple_of(me * FINE_B, 8), FINE_B), :]
         return carried
 
@@ -559,8 +570,6 @@
             states[1] = terms[0]
 
         def step(t, carried):
-            state_copy(t).start()
-
             def write_state(a, first, third):
                 if a == 0:
                     term_copy(t).wait_recv()
@@ -575,8 +584,10 @@
                 (out_f, in_f, out_b, in_b),
                 (f_send, f_recv, b_send, b_recv),
                 write_state,
+                compact=False,
             )
             begin()
+            state_copy(t).start()
             middle()
             end()
             return carried

time: 507 us -> 496 us (0.978)
  Pallas kernels: 504 us -> 493 us
    pallas_call x1, Pallas kernels: 504 us -> 493 us  [shards(): pl.pallas_call(partial(iteration_kernel, edges), out_shape=jax.ShapeDtype...]
where the time goes in v5:
time: 496 us
  Pallas kernels  493 us (99%)
    pallas_call x1, Pallas kernels, shards(): pl.pallas_call(partial(iteration_kernel, edges), out_shape=jax.ShapeDtype...  493 us

profile of v5, /device:TPU:103, one launch (start us, length us, event | category | flops | bytes accessed | tf_op | source)
XLA Modules:
  0.0 496.2 jit_solution(11840031001518482304)
XLA Ops:
  0.0 492.6 %shard_map.118 = f32[3,1024,128]{2,1,0:T(8,128)} custom-call(f32[3,1024,128]{2,1,0:T(8,128)} %bitcast.5, bf16[192,768]{1,0:T(8,128)(2,1)} %constant.27.clone.fine_spread, bf16[128,1152]{1,0:T(8,128)(2,1)} %constant.28.clone.fine_gather, bf16[2688,256]{1,0:T(8,128)(2,1)} %constant.34.deep, bf16[192,384]{1,0:T(8,128)(2,1)} %constant.35.coarse_spread, ...), custom_call_target="tpu_custom_call" | custom-call | tf_op jit(solution)/shard_map/pallas_call | solution.py:657
  492.6 3.6 copy.15

commit v6 on v5

--- a/solution.py
+++ b/solution.py
@@ -550,13 +550,20 @@
         device_id_type=MESH,
     )
 
-    @pl.when(sends_term)
+    late_term = sends_term & (slot >= 3) & jnp.logical_not(is_chain)
+
+    @pl.when(sends_term & jnp.logical_not(late_term))
     def _():
         term_copy(slot).start()
 
     @pl.when(slot < slices - 1)
     def _():
         end_copy.start()
+
+    @pl.when(late_term)
+    def _():
+        end_copy.wait_send()
+        term_copy(slot).start()
 
     @pl.when(is_chain)
     def _():
@@ -605,7 +612,7 @@
     def _():
         term_copy(slot).wait_send()
 
-    @pl.when(slot < slices - 1)
+    @pl.when((slot < slices - 1) & jnp.logical_not(late_term))
     def _():
         end_copy.wait_send()
 

time: 496 us -> 498 us (level)
  no operation moved by 1% of the time
where the time goes in v6:
time: 498 us
  Pallas kernels  494 us (99%)
    pallas_call x1, Pallas kernels, shards(): pl.pallas_call(partial(iteration_kernel, edges), out_shape=jax.ShapeDtype...  494 us

profile of v6, /device:TPU:103, one launch (start us, length us, event | category | flops | bytes accessed | tf_op | source)
XLA Modules:
  0.0 497.5 jit_solution(10766742678663238429)
XLA Ops:
  0.0 493.9 %shard_map.118 = f32[3,1024,128]{2,1,0:T(8,128)} custom-call(f32[3,1024,128]{2,1,0:T(8,128)} %bitcast.5, bf16[192,768]{1,0:T(8,128)(2,1)} %constant.27.clone.fine_spread, bf16[128,1152]{1,0:T(8,128)(2,1)} %constant.28.clone.fine_gather, bf16[2688,256]{1,0:T(8,128)(2,1)} %constant.34.deep, bf16[192,384]{1,0:T(8,128)(2,1)} %constant.35.coarse_spread, ...), custom_call_target="tpu_custom_call" | custom-call | tf_op jit(solution)/shard_map/pallas_call | solution.py:664
  493.9 3.6 copy.15
